TPU v7x, 64 devices: a 2x2x8 block of a 4x4x8 slice. The times are simulated.
64 devices in a mesh: dp: 4 (over x, y), cp: 16 (over z, core).
Axes of the slice: x: 2, y: 2, z: 8, core: 2. Of those that a mesh axis runs over, the one named last changes fastest.
The devices are a block of a 4x4x8 slice.
Arguments:
- x_in: bfloat16 [8192, 5120], P(('dp', 'cp')), parts along dimension 0
- d_y: bfloat16 [8192, 5120], P(('dp', 'cp')), parts along dimension 0
- w_q: bfloat16 [5120, 32, 128], replicated
- w_k: bfloat16 [5120, 8, 128], replicated
- w_v: bfloat16 [5120, 8, 128], replicated
- w_o: bfloat16 [32, 128, 5120], replicated
Outputs:
- output: bfloat16 [8192, 5120], P(('dp', 'cp')), parts along dimension 0
There are 4 independent parts. A program takes and returns all parts, laid end to end along the dimension named above; an argument that names none is the same for every part.
All inputs are finite; a program needn't handle non-finite values.
Results may differ from a plain program's by a relative error of at most 0.0114179.
Values are sent between devices in bfloat16 or wider.
A program may use at most 768 MiB of HBM per device.

v0:
```python
import math
import jax
import jax.numpy as jnp
from jax import lax
from jax.sharding import PartitionSpec as P


def block_rows(row_total, key_total, head_total):
    budget = max(1, 2 ** 23 // (key_total * head_total))
    return math.gcd(row_total, max(8, 2 ** int(math.log2(budget))))


def token_positions(row_ids, tok_len, n_dev):
    dev_idx = row_ids // tok_len
    row_off = row_ids % tok_len
    seg_len = tok_len // 2
    seg_idx = jnp.where(row_off < seg_len, dev_idx, 2 * n_dev - 1 - dev_idx)
    return seg_idx * seg_len + row_off % seg_len


def solution(mesh):
    n_dev = mesh.shape["cp"]
    row_spec = P(("dp", "cp"), None)

    def device_fn(x_in, d_y, w_q, w_k, w_v, w_o):
        tok_len, d_model = x_in.shape
        q_heads, head_dim = w_q.shape[1], w_q.shape[2]
        kv_heads = w_k.shape[1]
        q_group = q_heads // kv_heads
        seq_len = tok_len * n_dev
        score_scale = head_dim ** -0.5
        dev_rank = lax.axis_index("cp")
        wq_grp = w_q.reshape(d_model, kv_heads, q_group, head_dim)
        wo_grp = w_o.reshape(kv_heads, q_group, head_dim, d_model)
        q_loc = jnp.einsum("td,dkge->tkge", x_in, wq_grp, preferred_element_type=jnp.float32).astype(jnp.bfloat16)
        k_loc = jnp.einsum("td,dke->tke", x_in, w_k, preferred_element_type=jnp.float32).astype(jnp.bfloat16)
        v_loc = jnp.einsum("td,dke->tke", x_in, w_v, preferred_element_type=jnp.float32).astype(jnp.bfloat16)
        do_loc = jnp.einsum("td,kged->tkge", d_y, wo_grp, preferred_element_type=jnp.float32).astype(jnp.bfloat16)
        k_all = lax.all_gather(k_loc, "cp", axis=0, tiled=True)
        v_all = lax.all_gather(v_loc, "cp", axis=0, tiled=True)
        pos_all = token_positions(jnp.arange(seq_len), tok_len, n_dev)
        pos_loc = token_positions(dev_rank * tok_len + jnp.arange(tok_len), tok_len, n_dev)
        blk_rows = block_rows(tok_len, seq_len, q_heads)

        def block_step(acc_pair, blk_idx):
            dk_acc, dv_acc = acc_pair
            row_start = blk_idx * blk_rows
            q_blk = lax.dynamic_slice_in_dim(q_loc, row_start, blk_rows, 0)
            do_blk = lax.dynamic_slice_in_dim(do_loc, row_start, blk_rows, 0)
            pos_blk = lax.dynamic_slice_in_dim(pos_loc, row_start, blk_rows, 0)
            scores = jnp.einsum("rkge,ske->krgs", q_blk, k_all, preferred_element_type=jnp.float32) * score_scale
            causal = pos_blk[None, :, None, None] >= pos_all[None, None, None, :]
            scores = jnp.where(causal, scores, -jnp.inf)
            lse_blk = jax.nn.logsumexp(scores, axis=-1, keepdims=True)
            prob_blk = jnp.exp(scores - lse_blk).astype(jnp.bfloat16)
            out_blk = jnp.einsum("krgs,ske->krge", prob_blk, v_all, preferred_element_type=jnp.float32).astype(jnp.bfloat16)
            row_delta = jnp.einsum("rkge,krge->krg", do_blk, out_blk, preferred_element_type=jnp.float32)
            dp_blk = jnp.einsum("rkge,ske->krgs", do_blk, v_all, preferred_element_type=jnp.float32)
            ds_blk = (prob_blk * (dp_blk - row_delta[..., None])).astype(jnp.bfloat16)
            dq_blk = (jnp.einsum("krgs,ske->krge", ds_blk, k_all, preferred_element_type=jnp.float32) * score_scale).astype(jnp.bfloat16)
            dk_acc = dk_acc + jnp.einsum("krgs,rkge->kse", ds_blk, q_blk, preferred_element_type=jnp.float32)
            dv_acc = dv_acc + jnp.einsum("krgs,rkge->kse", prob_blk, do_blk, preferred_element_type=jnp.float32)
            return (dk_acc, dv_acc), dq_blk

        zero_acc = jnp.zeros((kv_heads, seq_len, head_dim), jnp.float32)
        (dk_part, dv_part), dq_blocks = lax.scan(block_step, (zero_acc, zero_acc), jnp.arange(tok_len // blk_rows))
        d_key = lax.psum_scatter(dk_part * score_scale, "cp", scatter_dimension=1, tiled=True).astype(jnp.bfloat16)
        d_value = lax.psum_scatter(dv_part, "cp", scatter_dimension=1, tiled=True).astype(jnp.bfloat16)
        d_x = jnp.einsum("bkrge,dkge->brd", dq_blocks, wq_grp, preferred_element_type=jnp.float32).reshape(tok_len, d_model)
        d_x = d_x + jnp.einsum("kte,dke->td", d_key, w_k, preferred_element_type=jnp.float32)
        d_x = d_x + jnp.einsum("kte,dke->td", d_value, w_v, preferred_element_type=jnp.float32)
        return d_x.astype(jnp.bfloat16)

    return jax.shard_map(device_fn, mesh=mesh, in_specs=(row_spec, row_spec, P(), P(), P(), P()), out_specs=row_spec, check_vma=False)
```

profile of v0, /device:TPU:21, one launch (start us, length us, event | category | flops | bytes accessed | tf_op | source)
XLA Modules:
  0.0 299.6 jit_solution(6082657232226296364)
XLA Ops:
  6.6 6.8 %fusion.50 = bf16[128,8,128]{2,0,1:T(8,128)(2,1)} fusion(bf16[5120,8,128]{2,1,0:T(8,128)(2,1)} %param.9, bf16[128,5120]{1,0:T(8,128)(2,1)} %param.6), kind=kOutput, calls=%fused_computation.42 | convolution fusion | flops 1342308352 | bytes 12058624 | tf_op jit(solution)/shard_map/td,dke->tke/dot_general | solution.py:36
  13.4 0.1 all-gather.5.cloned.1.call-start
  13.5 6.2 %fusion.55 = bf16[128,8,128]{2,0,1:T(8,128)(2,1)} fusion(bf16[5120,8,128]{2,1,0:T(8,128)(2,1)} %param.10, bf16[128,5120]{1,0:T(8,128)(2,1)S(1)} %copy-done.4), kind=kOutput, calls=%fused_computation.43 | convolution fusion | flops 1342308352 | bytes 12058624 | tf_op jit(solution)/shard_map/td,dke->tke/dot_general | solution.py:37
  19.7 0.6 reduce-scatter.3.cloned.1.call-start
  20.4 19.2 %fusion.43 = bf16[128,8,4,128]{3,0,2,1:T(8,128)(2,1)S(1)} fusion(bf16[5120,8,4,128]{3,2,1,0:T(4,128)(2,1)} %bitcast.79, bf16[128,5120]{1,0:T(8,128)(2,1)} %param.6), kind=kOutput, calls=%fused_computation.36 | convolution fusion | flops 5369233408 | bytes 44302336 | tf_op jit(solution)/shard_map/td,dkge->tkge/dot_general | solution.py:35
  39.6 20.1 %bitcast_convert_fusion = (f32[8,128,4,128]{3,1,2,0:T(8,128)}, bf16[128,8,4,128]{3,0,2,1:T(8,128)(2,1)S(1)}) fusion(bf16[8,4,128,5120]{3,2,1,0:T(8,128)(2,1)} %bitcast.78, bf16[128,5120]{1,0:T(8,128)(2,1)S(1)} %copy-done), kind=kOutput, calls=%fused_computation.44 | convolution fusion | flops 5369757696 | bytes 46399488 | tf_op jit(solution)/shard_map/td,kged->tkge/dot_general | solution.py:38
  59.7 0.2 broadcast_compare_fusion
  60.0 15.8 %fusion.4 = (f32[8,128,4]{1,2,0:T(4,128)S(1)}, f32[8,128,4,2048]{3,1,2,0:T(8,128)}) fusion(pred[128,2048]{1,0:T(8,128)(4,1)S(1)} %broadcast_compare_fusion, bf16[128,8,4,128]{3,0,2,1:T(8,128)(2,1)S(1)} %fusion.43, bf16[2048,8,128]{2,0,1:T(8,128)(2,1)} %all-gather.3.cloned.1.call-done), kind=kOutput, calls=%fused_computation.8 | convolution fusion | flops 2172645376 | bytes 39075840 | tf_op jit(solution)/shard_map/while/body/eval_jaxpr/rkge,ske->krgs/dot_general | solution.py:51
  75.7 16.6 %exponential_reduce_fusion = f32[8,128,4]{1,2,0:T(4,128)S(1)} fusion(f32[8,128,4,2048]{3,1,2,0:T(8,128)} %get-tuple-element.24, f32[8,128,4]{1,2,0:T(4,128)S(1)} %is-finite_select_fusion, pred[128,2048]{1,0:T(8,128)(4,1)S(1)} %broadcast_compare_fusion), kind=kLoop, calls=%fused_computation.6 | loop fusion | flops 33550336 | bytes 33849344 | tf_op jit(solution)/shard_map/while/body/eval_jaxpr/reduce_sum | solution.py:54
  92.4 3.6 %copy-done.2 = f32[8,128,4,2048]{3,1,2,0:T(8,128)S(1)} copy-done((f32[8,128,4,2048]{3,1,2,0:T(8,128)S(1)}, f32[8,128,4,2048]{3,1,2,0:T(8,128)}, u32[]{:S(2)}) %copy-start.2) | copy-done | bytes 33554456
  96.0 9.5 %exponential_convert_fusion = bf16[8,128,4,2048]{3,1,2,0:T(8,128)(2,1)} fusion(f32[8,128,4,2048]{3,1,2,0:T(8,128)S(1)} %copy-done.2, f32[8,128,4]{1,2,0:T(4,128)S(1)} %log_add_fusion, pred[128,2048]{1,0:T(8,128)(4,1)S(1)} %broadcast_compare_fusion), kind=kLoop, calls=%fused_computation.5 | loop fusion | flops 33554432 | bytes 50610176 | tf_op jit(solution)/shard_map/while/body/eval_jaxpr/convert_element_type | solution.py:55
  105.5 11.6 %fusion.35 = bf16[8,128,4,128]{3,1,2,0:T(8,128)(2,1)S(1)} fusion(bf16[8,128,4,2048]{3,1,2,0:T(8,128)(2,1)} %exponential_convert_fusion, bf16[2048,8,128]{2,0,1:T(8,128)(2,1)} %all-gather.5.cloned.1.call-done), kind=kOutput, calls=%fused_computation.29 | convolution fusion | flops 2147483648 | bytes 22020096 | tf_op jit(solution)/shard_map/while/body/eval_jaxpr/krgs,ske->krge/dot_general | solution.py:56
  117.1 2.1 multiply_reduce_fusion
  119.2 0.2 copy.23
  119.4 14.3 %multiply_convert_fusion = bf16[8,128,4,2048]{3,1,2,0:T(8,128)(2,1)} fusion(bf16[8,128,4,2048]{3,1,2,0:T(8,128)(2,1)} %exponential_convert_fusion, bf16[128,8,4,128]{3,0,2,1:T(8,128)(2,1)S(1)} %get-tuple-element.26, f32[8,128,4]{1,2,0:T(4,128)S(1)} %copy.23, bf16[2048,8,128]{2,0,1:T(8,128)(2,1)} %all-gather.5.cloned.1.call-done), kind=kOutput, calls=%fused_computation.4 | convolution fusion | flops 2181038080 | bytes 38813696 | tf_op jit(solution)/shard_map/while/body/eval_jaxpr/rkge,ske->krgs/dot_general | solution.py:58
  133.7 11.4 %bitcast_multiply_fusion = f32[8,2048,128]{2,1,0:T(8,128)} fusion(bf16[8,128,4,2048]{3,1,2,0:T(8,128)(2,1)} %multiply_convert_fusion, bf16[128,8,4,128]{3,0,2,1:T(8,128)(2,1)S(1)} %fusion.43), kind=kOutput, calls=%fused_computation.19 | convolution fusion | flops 2149580800 | bytes 26214400 | tf_op jit(solution)/shard_map/while/body/eval_jaxpr/krgs,rkge->kse/dot_general | solution.py:61
  145.2 0.1 reduce-scatter.5.cloned.1.call-start
  145.3 11.6 %convolution_bitcast_fusion = f32[8,2048,128]{2,1,0:T(8,128)} fusion(bf16[8,128,4,2048]{3,1,2,0:T(8,128)(2,1)} %exponential_convert_fusion, bf16[128,8,4,128]{3,0,2,1:T(8,128)(2,1)S(1)} %get-tuple-element.26), kind=kOutput, calls=%fused_computation.26 | convolution fusion | flops 2147483648 | bytes 26214400 | tf_op jit(solution)/shard_map/while/body/eval_jaxpr/krgs,rkge->kse/dot_general | solution.py:62
  157.0 11.4 %multiply_convert_fusion.1.clone.4 = bf16[8,128,4,128]{3,1,0,2:T(8,128)(2,1)S(1)} fusion(bf16[2048,8,128]{2,0,1:T(8,128)(2,1)} %all-gather.3.cloned.1.call-done, bf16[8,128,4,2048]{3,1,2,0:T(8,128)(2,1)} %multiply_convert_fusion), kind=kOutput, calls=%fused_computation.35.clone.clone.clone.1 | convolution fusion | flops 2148532224 | bytes 22020096 | tf_op jit(solution)/shard_map/while/body/eval_jaxpr/krgs,ske->krge/dot_general | solution.py:60
  168.4 24.4 %fusion.15 = f32[128,5120]{1,0:T(8,128)} fusion(bf16[5120,8,4,128]{3,2,1,0:T(4,128)(2,1)} %bitcast.80, bf16[8,128,4,128]{3,1,0,2:T(8,128)(2,1)S(1)} %multiply_convert_fusion.1.clone.4), kind=kOutput, calls=%fused_computation.20 | convolution fusion | flops 5368709120 | bytes 45613056 | tf_op jit(solution)/shard_map/bkrge,dkge->brd/dot_general | solution.py:69
  192.8 21.9 %reduce-scatter.3.cloned.1.call-done = f32[8,128,128]{2,1,0:T(8,128)} async-done(((f32[8,2048,128]{2,1,0:T(8,128)}), f32[8,128,128]{2,1,0:T(8,128)}) %reduce-scatter.3.cloned.1.call-update) | async-done | bytes 524304 | tf_op jit(solution)/shard_map/reduce_scatter | solution.py:67
  214.7 10.1 %fusion.27 = f32[128,5120]{1,0:T(8,128)} fusion(f32[128,5120]{1,0:T(8,128)} %fusion.15, bf16[5120,8,128]{2,1,0:T(8,128)(2,1)} %param.9, f32[8,128,128]{2,1,0:T(8,128)} %reduce-scatter.3.cloned.1.call-done), kind=kOutput, calls=%fused_computation.24 | convolution fusion | flops 1342963712 | bytes 16252928 | tf_op jit(solution)/shard_map/kte,dke->td/dot_general | solution.py:70
  224.7 58.5 %reduce-scatter.5.cloned.1.call-done = f32[8,128,128]{2,1,0:T(8,128)} async-done(((f32[8,2048,128]{2,1,0:T(8,128)}), f32[8,128,128]{2,1,0:T(8,128)}) %reduce-scatter.5.cloned.1.call-update) | async-done | bytes 524304 | tf_op jit(solution)/shard_map/reduce_scatter | solution.py:68
  283.3 9.5 %fusion.30 = bf16[128,5120]{1,0:T(8,128)(2,1)} fusion(f32[128,5120]{1,0:T(8,128)} %fusion.27, bf16[5120,8,128]{2,1,0:T(8,128)(2,1)} %param.10, f32[8,128,128]{2,1,0:T(8,128)} %reduce-scatter.5.cloned.1.call-done), kind=kOutput, calls=%fused_computation.25 | convolution fusion | flops 1343619072 | bytes 14942208 | tf_op jit(solution)/shard_map/kte,dke->td/dot_general | solution.py:71
  (20 shorter events, 0.3 us)
Async XLA Ops:
  6.5 33.1 %copy-start = (bf16[128,5120]{1,0:T(8,128)(2,1)S(1)}, bf16[128,5120]{1,0:T(8,128)(2,1)}, u32[]{:S(2)}) copy-start(bf16[128,5120]{1,0:T(8,128)(2,1)} %param.7) | copy-start | bytes 3932164
  6.6 6.9 %copy-start.4 = (bf16[128,5120]{1,0:T(8,128)(2,1)S(1)}, bf16[128,5120]{1,0:T(8,128)(2,1)}, u32[]{:S(2)}) copy-start(bf16[128,5120]{1,0:T(8,128)(2,1)} %param.6) | copy-start | bytes 3932164
  6.6 53.4 %all-gather.3.cloned.1.call-start = ((), (), s32[]{:S(2)}) async-start(), calls=%async_computation.2 | async-start | bytes 4456448 | tf_op jit(solution)/shard_map/all_gather | solution.py:39
  13.4 92.1 %all-gather.5.cloned.1.call-start = ((), (), s32[]{:S(2)}) async-start(), calls=%async_computation.3 | async-start | bytes 4456448 | tf_op jit(solution)/shard_map/all_gather | solution.py:40
  19.7 194.9 %reduce-scatter.3.cloned.1.call-start = ((), (), s32[]{:S(2)}) async-start(), calls=%async_computation.4 | async-start | bytes 8912896 | tf_op jit(solution)/shard_map/reduce_scatter | solution.py:67
  75.7 20.2 %copy-start.2 = (f32[8,128,4,2048]{3,1,2,0:T(8,128)S(1)}, f32[8,128,4,2048]{3,1,2,0:T(8,128)}, u32[]{:S(2)}) copy-start(f32[8,128,4,2048]{3,1,2,0:T(8,128)} %get-tuple-element.24) | copy-start | bytes 100663296
  105.5 11.6 %copy-start.3 = (f32[8,128,4,128]{3,1,2,0:T(8,128)S(1)}, f32[8,128,4,128]{3,1,2,0:T(8,128)}, u32[]{:S(2)}) copy-start(f32[8,128,4,128]{3,1,2,0:T(8,128)} %get-tuple-element.25) | copy-start | bytes 6291460
  145.2 138.1 %reduce-scatter.5.cloned.1.call-start = ((), (), s32[]{:S(2)}) async-start(), calls=%async_computation.5 | async-start | bytes 8912896 | tf_op jit(solution)/shard_map/reduce_scatter | solution.py:68
  214.7 78.1 %copy-start.1 = (bf16[128,5120]{1,0:T(8,128)(2,1)S(1)}, bf16[128,5120]{1,0:T(8,128)(2,1)}, u32[]{:S(2)}) copy-start(bf16[128,5120]{1,0:T(8,128)(2,1)} %param.7) | copy-start | bytes 3932164
Sparse Core Ops, SparseCore 0:
  13.5 43.6 all-gather.2
  58.8 36.9 all-gather.4
  145.3 69.3 reduce-scatter.2
  216.9 66.3 reduce-scatter.4
where the time goes:
time: 305 us; the launch traced here: 300 us
  matrix products  172 us (56%)
  waiting for transfers between devices  80.6 us (26%)
  other arithmetic  28.4 us (9%)
  between operations  13.5 us (4%)
  local copies, waits for them, and re-layouts  3.79 us (1%)
    reduce_scatter x1, waiting for transfers between devices, device_fn(): lax.psum_scatter(dv_part, 'cp', scatter_dimension=1, tiled=True)  58.5 us
    dot_general x1, matrix products, device_fn(): jnp.einsum('bkrge,dkge->brd', dq_blocks, wq_grp, preferred_element_type=j...  24.4 us
    reduce_scatter x1, waiting for transfers between devices, device_fn(): lax.psum_scatter(dk_part * score_scale, 'cp', scatter_dimension=1, tiled=...  21.9 us
    dot_general x1, matrix products, device_fn(): jnp.einsum('td,kged->tkge', d_y, wo_grp, preferred_element_type=jnp.float32)  20.1 us
    dot_general x1, matrix products, device_fn(): jnp.einsum('td,dkge->tkge', x_in, wq_grp, preferred_element_type=jnp.floa...  19.2 us
    reduce_sum x1, other arithmetic, block_step(): lse_blk = jax.nn.logsumexp(scores, axis=-1, keepdims=True)  16.6 us
    dot_general x1, matrix products, block_step(): jnp.einsum('rkge,ske->krgs', q_blk, k_all, preferred_element_type=jnp.flo...  15.8 us
    dot_general x1, matrix products, block_step(): jnp.einsum('rkge,ske->krgs', do_blk, v_all, preferred_element_type=jnp.fl...  14.3 us
  transfers between devices with their start and end apart: 4, of which 2 were waited for; matrix products, arithmetic and copies ran while one was open for 48% of the time, Pallas kernels for 0%

commit v1 on v0

v1 whole, which is shorter than its diff:
```python
import functools

import jax
import jax.numpy as jnp
from jax import lax
from jax.experimental import pallas as pl
from jax.experimental.pallas import tpu as pltpu
from jax.sharding import PartitionSpec as P

MESH = pl.DeviceIdType.MESH
BF16 = jnp.bfloat16
F32 = jnp.float32
CONTRACT_LAST = (((1,), (1,)), ((), ()))
DEPTH = 4
WO_DEPTH = 3
D_CHUNK = 512
VMEM_LIMIT = 62 * 2 ** 20


def place():
    me = lax.axis_index("cp")
    chip = me // 2
    core = me % 2
    return me, chip, core, me + 1 - 2 * core


def meet_group(n_dev):
    me = lax.axis_index("cp")
    barrier = pltpu.get_barrier_semaphore()

    def greet(step, carry):
        other = lax.rem(me + step, n_dev)
        pl.semaphore_signal(barrier, inc=1, device_id={"cp": other}, device_id_type=MESH)
        return carry

    lax.fori_loop(1, n_dev, greet, 0)
    pl.semaphore_wait(barrier, n_dev - 1)


def rcopy(src, dst, send_sem, recv_sem, dev):
    return pltpu.make_async_remote_copy(
        src_ref=src, dst_ref=dst, send_sem=send_sem, recv_sem=recv_sem,
        device_id={"cp": dev}, device_id_type=MESH)


def al(value, step):
    return pl.multiple_of(value, step)


def ship_start(is_me, src, dst, send_sem, recv_sem, dev):
    @pl.when(is_me)
    def _():
        pltpu.make_async_copy(src, dst, send_sem).start()

    @pl.when(jnp.logical_not(is_me))
    def _():
        rcopy(src, dst, send_sem, recv_sem, dev).start()


def ship_wait(is_me, src, dst, send_sem, recv_sem, dev):
    @pl.when(is_me)
    def _():
        pltpu.make_async_copy(src, dst, send_sem).wait()

    @pl.when(jnp.logical_not(is_me))
    def _():
        rcopy(src, dst, send_sem, recv_sem, dev).wait_send()


def project_kernel(n_dev, x_ref, dy_ref, wq, wk, wv, wo, q_all, do_all, kv_all,
                   xs, dys, wo_buf, w_buf, acc, st_do, st_kv, st_q,
                   wo_sem, w_sem, x_send, x_recv, do_send, do_recv,
                   kv_send, kv_recv, q_send, q_recv, rel_send, rel_recv):
    me, chip, core, sib = place()
    n_chip = n_dev // 2
    rows, d_model = x_ref.shape
    seg = rows // 2
    head = kv_all.shape[2]
    wide = q_all.shape[1]
    tile_w = acc.shape[1]
    n_chunk = d_model // D_CHUNK
    n_dest = n_dev // 2
    tile_heads = w_buf.shape[2]
    my_src_core = chip // (n_chip // 2)
    low_at = al(chip * rows, rows)
    high_at = al((2 * n_chip - 1 - chip) * rows, rows)

    def dest_of(n):
        return n_dest * core + lax.rem(n + 2 * chip, n_dest)

    def wo_copy(n):
        return pltpu.make_async_copy(
            wo.at[pl.ds(al(dest_of(n) * wide, wide), wide), :], wo_buf.at[lax.rem(n, WO_DEPTH)],
            wo_sem.at[lax.rem(n, WO_DEPTH)])

    def tile_of(t):
        return 2 * core + lax.rem(t + chip // 2, 2)

    def w_start(s):
        slot = lax.rem(s, DEPTH)
        part = lax.rem(s, n_chunk)
        d_rows = pl.ds(al(part * D_CHUNK, D_CHUNK), D_CHUNK)

        @pl.when((s < n_chunk) & (core == 0))
        def _():
            pltpu.make_async_copy(wk.at[d_rows], w_buf.at[slot], w_sem.at[slot]).start()

        @pl.when((s < n_chunk) & (core == 1))
        def _():
            pltpu.make_async_copy(wv.at[d_rows], w_buf.at[slot], w_sem.at[slot]).start()

        @pl.when((s >= n_chunk) & (s < 3 * n_chunk))
        def _():
            tile = tile_of(s // n_chunk - 1)
            pltpu.make_async_copy(
                wq.at[d_rows, pl.ds(al(tile * tile_heads, tile_heads), tile_heads), :],
                w_buf.at[slot], w_sem.at[slot]).start()

    def w_wait(s):
        slot = lax.rem(s, DEPTH)
        pltpu.make_async_copy(wk.at[pl.ds(0, D_CHUNK)], w_buf.at[slot], w_sem.at[slot]).wait()

    for n in range(WO_DEPTH - 1):
        wo_copy(n).start()
    for s in range(DEPTH - 1):
        w_start(s)

    my_low = al(core * seg, seg)
    my_high = al(rows + (1 - core) * seg, seg)
    for ref, stack in ((dy_ref, dys), (x_ref, xs)):
        stack[pl.ds(my_low, seg), :] = ref[:seg, :]
        stack[pl.ds(my_high, seg), :] = ref[seg:, :]
    meet_group(n_dev)
    swaps = []
    for k, (ref, stack) in enumerate(((dy_ref, dys), (x_ref, xs))):
        swaps.append(rcopy(ref.at[pl.ds(0, seg)], stack.at[pl.ds(my_low, seg)],
                           x_send.at[k, 0], x_recv.at[k, 0], sib))
        swaps.append(rcopy(ref.at[pl.ds(seg, seg)], stack.at[pl.ds(my_high, seg)],
                           x_send.at[k, 1], x_recv.at[k, 1], sib))
    for swap in swaps:
        swap.start()
    swaps[0].wait()
    swaps[1].wait()

    def do_ship(n, act):
        dest = dest_of(n)
        for k, at in enumerate((low_at, high_at)):
            act(dest == me, st_do.at[n, pl.ds(k * rows, rows), :], do_all.at[pl.ds(at, rows), :],
                do_send.at[n, k], do_recv.at[chip, k], dest)

    def do_step(n, carry):
        @pl.when(n + WO_DEPTH - 1 < n_dest)
        def _():
            wo_copy(n + WO_DEPTH - 1).start()
        wo_copy(n).wait()

        @pl.when(n > 0)
        def _():
            do_ship(n - 1, ship_start)
        st_do[n] = lax.dot_general(dys[...], wo_buf[lax.rem(n, WO_DEPTH)], CONTRACT_LAST,
                                   preferred_element_type=F32).astype(BF16)
        return carry

    lax.fori_loop(0, n_dest, do_step, 0)
    swaps[2].wait()
    swaps[3].wait()

    def w_step(s, first):
        w_start(s + DEPTH - 1)
        w_wait(s)
        part = lax.rem(s, n_chunk)
        w_tile = w_buf[lax.rem(s, DEPTH)].reshape(D_CHUNK, tile_w)
        add = jnp.dot(xs[:, pl.ds(al(part * D_CHUNK, D_CHUNK), D_CHUNK)], w_tile,
                      preferred_element_type=F32)
        acc[...] = add if first else acc[...] + add

    def w_loop(lo, hi):
        def body(s, carry):
            w_step(s, False)
            return carry
        lax.fori_loop(lo, hi, body, 0)

    def kv_ship(dest_chip, act):
        dest = 2 * dest_chip + core
        lanes = pl.ds(al(dest_chip * head, head), head)
        for k, at in enumerate((low_at, high_at)):
            act(dest == me, st_kv.at[pl.ds(k * rows, rows), lanes], kv_all.at[core, pl.ds(at, rows), :],
                kv_send.at[dest_chip, k], kv_recv.at[chip, k], dest)

    def kv_ship_all(act):
        def body(n, carry):
            kv_ship(lax.rem(n + chip, n_chip), act)
            return carry
        lax.fori_loop(0, n_chip, body, 0)

    def q_ship(t, n, act):
        dest = 4 * tile_of(t) + lax.rem(n + 2 * chip, 4)
        lanes = pl.ds(al(lax.rem(dest, 4) * wide, wide), wide)
        for k, at in enumerate((low_at, high_at)):
            act(dest == me, st_q.at[t, pl.ds(k * rows, rows), lanes], q_all.at[pl.ds(at, rows), :],
                q_send.at[4 * t + n, k], q_recv.at[chip, k], dest)

    def q_ship_all(t, act):
        def body(n, carry):
            q_ship(t, n, act)
            return carry
        lax.fori_loop(0, 4, body, 0)

    w_step(0, True)
    do_ship(n_dest - 1, ship_start)
    w_loop(1, n_chunk)
    st_kv[...] = acc[...].astype(BF16)
    w_step(n_chunk, True)
    kv_ship_all(ship_start)
    w_loop(n_chunk + 1, 2 * n_chunk)
    st_q[0] = acc[...].astype(BF16)
    w_step(2 * n_chunk, True)
    q_ship_all(0, ship_start)
    w_loop(2 * n_chunk + 1, 3 * n_chunk)
    st_q[1] = acc[...].astype(BF16)

    def kv_arrive(src_chip, carry):
        @pl.when(src_chip != chip)
        def _():
            for k in range(2):
                rcopy(st_kv.at[pl.ds(0, rows), pl.ds(0, head)], kv_all.at[core, pl.ds(0, rows), :],
                      kv_send.at[0, k], kv_recv.at[src_chip, k], sib).wait_recv()
        return carry

    lax.fori_loop(0, n_chip, kv_arrive, 0)
    q_ship_all(1, ship_start)
    kv_ship_all(ship_wait)
    relay = rcopy(kv_all.at[core], kv_all.at[core], rel_send, rel_recv, sib)
    relay.start()

    def wide_arrive(src_chip, carry):
        @pl.when(2 * src_chip + my_src_core != me)
        def _():
            for k in range(2):
                rcopy(st_do.at[0, pl.ds(0, rows), :], do_all.at[pl.ds(0, rows), :],
                      do_send.at[0, k], do_recv.at[src_chip, k], sib).wait_recv()
                rcopy(st_do.at[0, pl.ds(0, rows), :], q_all.at[pl.ds(0, rows), :],
                      q_send.at[0, k], q_recv.at[src_chip, k], sib).wait_recv()
        return carry

    lax.fori_loop(0, n_chip, wide_arrive, 0)

    def do_done(n, carry):
        do_ship(n, ship_wait)
        return carry

    lax.fori_loop(0, n_dest, do_done, 0)
    q_ship_all(0, ship_wait)
    q_ship_all(1, ship_wait)
    rcopy(kv_all.at[core], kv_all.at[1 - core], rel_send, rel_recv, sib).wait_recv()
    relay.wait_send()


def attend_kernel(scale, q_ref, do_ref, kv_ref, dq_ref, dkv_ref, k_t, v_t, s_scr, p_scr):
    seq, wide = q_ref.shape
    head = kv_ref.shape[2]
    heads = wide // head
    bq, bk = 256, 512
    k_t[...] = kv_ref[0].T
    v_t[...] = kv_ref[1].T
    dkv_ref[...] = jnp.zeros_like(dkv_ref)
    to_log2 = scale * 1.4426950408889634

    def q_block(qb, carry):
        q_rows = pl.ds(al(qb * bq, bq), bq)
        q = [q_ref[q_rows, h * head:(h + 1) * head] for h in range(heads)]
        do = [do_ref[q_rows, h * head:(h + 1) * head] for h in range(heads)]
        last = (qb * bq) // bk

        def keys(kc):
            return pl.ds(al(kc * bk, bk), bk)

        def scores(kc, tops, masked):
            k_blk = kv_ref[0, keys(kc), :]
            out = []
            for h in range(heads):
                s = lax.dot_general(k_blk, q[h], CONTRACT_LAST, preferred_element_type=F32)
                if masked:
                    k_pos = kc * bk + lax.broadcasted_iota(jnp.int32, (bk, bq), 0)
                    q_pos = qb * bq + lax.broadcasted_iota(jnp.int32, (bk, bq), 1)
                    s = jnp.where(k_pos <= q_pos, s, -jnp.inf)
                s_scr[h, keys(kc), :] = s
                out.append(jnp.maximum(tops[h], jnp.max(s, axis=0, keepdims=True)))
            return tuple(out)

        tops = tuple(jnp.full((1, bq), -jnp.inf, F32) for _ in range(heads))
        tops = lax.fori_loop(0, last, lambda kc, c: scores(kc, c, False), tops)
        tops = scores(last, tops, True)
        tops = [t * to_log2 for t in tops]

        def expo(kc, sums):
            out = []
            for h in range(heads):
                e = jnp.exp2(s_scr[h, keys(kc), :] * to_log2 - tops[h])
                s_scr[h, keys(kc), :] = e
                out.append(sums[h] + jnp.sum(e, axis=0, keepdims=True))
            return tuple(out)

        sums = lax.fori_loop(0, last + 1, expo, tuple(jnp.zeros((1, bq), F32) for _ in range(heads)))
        inv = [1.0 / s for s in sums]

        def outs(kc, acc):
            v_blk = v_t[:, keys(kc)]
            out = []
            for h in range(heads):
                p = (s_scr[h, keys(kc), :] * inv[h]).astype(BF16)
                p_scr[h, keys(kc), :] = p
                out.append(acc[h] + jnp.dot(v_blk, p, preferred_element_type=F32))
            return tuple(out)

        zero = tuple(jnp.zeros((head, bq), F32) for _ in range(heads))
        o_t = lax.fori_loop(0, last + 1, outs, zero)
        delta = [jnp.sum(do[h].astype(F32).T * o_t[h].astype(BF16).astype(F32), axis=0, keepdims=True)
                 for h in range(heads)]

        def grads(kc, acc):
            k_blk = k_t[:, keys(kc)]
            v_blk = kv_ref[1, keys(kc), :]
            out = []
            dk = dv = None
            for h in range(heads):
                p = p_scr[h, keys(kc), :]
                dp = lax.dot_general(v_blk, do[h], CONTRACT_LAST, preferred_element_type=F32)
                ds = (p.astype(F32) * (dp - delta[h])).astype(BF16)
                out.append(acc[h] + jnp.dot(k_blk, ds, preferred_element_type=F32))
                dk_h = jnp.dot(ds, q[h], preferred_element_type=F32)
                dv_h = jnp.dot(p, do[h], preferred_element_type=F32)
                dk = dk_h if dk is None else dk + dk_h
                dv = dv_h if dv is None else dv + dv_h
            dkv_ref[0, keys(kc), :] += dk
            dkv_ref[1, keys(kc), :] += dv
            return tuple(out)

        dq_t = lax.fori_loop(0, last + 1, grads, zero)
        for h in range(heads):
            dq_ref[q_rows, h * head:(h + 1) * head] = (dq_t[h] * scale).T.astype(BF16)
        return carry

    lax.fori_loop(0, seq // bq, q_block, 0)


def collect_kernel(n_dev, scale, dq_ref, dkv_ref, wq, wk, wv, dx_ref,
                   dq_in, dkv_in, dkv_far, dkv_st, w_buf, w2, acc, far,
                   w_sem, dq_send, dq_recv, dkv_send, dkv_recv, far_send, far_recv, red_send, red_recv):
    me, chip, core, sib = place()
    n_chip = n_dev // 2
    rows, d_model = dx_ref.shape
    seg = rows // 2
    head = dkv_ref.shape[2]
    wide = dq_ref.shape[1]
    n_chunk = d_model // D_CHUNK
    tile_heads = w_buf.shape[2]
    tile_w = w2.shape[2]
    half_dev = n_dev // 2
    dq_core = chip // (n_chip // 2)

    def w_start(s):
        slot = lax.rem(s, DEPTH)
        part = lax.rem(s, n_chunk)
        d_rows = pl.ds(al(part * D_CHUNK, D_CHUNK), D_CHUNK)

        @pl.when(s < 2 * n_chunk)
        def _():
            tile = 2 * core + s // n_chunk
            pltpu.make_async_copy(
                wq.at[d_rows, pl.ds(al(tile * tile_heads, tile_heads), tile_heads), :],
                w_buf.at[slot], w_sem.at[slot]).start()

        @pl.when((s >= 2 * n_chunk) & (s < 3 * n_chunk) & (core == 0))
        def _():
            pltpu.make_async_copy(wk.at[d_rows], w_buf.at[slot], w_sem.at[slot]).start()

        @pl.when((s >= 2 * n_chunk) & (s < 3 * n_chunk) & (core == 1))
        def _():
            pltpu.make_async_copy(wv.at[d_rows], w_buf.at[slot], w_sem.at[slot]).start()

    for s in range(DEPTH - 1):
        w_start(s)
    meet_group(n_dev)
    swap = rcopy(dkv_ref.at[1 - core], dkv_far, red_send, red_recv, sib)
    swap.start()

    src_slot = lax.rem(me, half_dev)

    def at_of(dest_chip, k):
        block = dest_chip if k == 0 else 2 * n_chip - 1 - dest_chip
        return al(block * rows, rows)

    def dq_ship(n, act):
        dest_chip = lax.rem(chip + n, n_chip)
        dest = 2 * dest_chip + dq_core
        for k in range(2):
            act(dest == me, dq_ref.at[pl.ds(at_of(dest_chip, k), rows), :],
                dq_in.at[src_slot // 4, pl.ds(k * rows, rows), pl.ds(al(lax.rem(src_slot, 4) * wide, wide), wide)],
                dq_send.at[n, k], dq_recv.at[src_slot, k], dest)

    def dkv_ship(n, act):
        dest_chip = lax.rem(chip + n, n_chip)
        dest = 2 * dest_chip + core
        for k in range(2):
            act(dest == me, dkv_st.at[pl.ds(at_of(dest_chip, k), rows), :],
                dkv_in.at[pl.ds(k * rows, rows), pl.ds(al(chip * head, head), head)],
                dkv_send.at[n, k], dkv_recv.at[chip, k], dest)

    def each(ship, act):
        def body(n, carry):
            ship(n, act)
            return carry
        lax.fori_loop(0, n_chip, body, 0)

    each(dq_ship, ship_start)
    swap.wait()
    factor = jnp.where(core == 0, scale, 1.0).astype(F32)
    dkv_st[...] = ((dkv_ref[core] + dkv_far[...]) * factor).astype(BF16)

    def turn(s, carry):
        w_start(s + DEPTH - 1)
        slot = lax.rem(s, DEPTH)
        pltpu.make_async_copy(wk.at[pl.ds(0, D_CHUNK)], w_buf.at[slot], w_sem.at[slot]).wait()
        w2[s] = w_buf[slot].reshape(D_CHUNK, tile_w)
        return carry

    turn(0, 0)
    each(dkv_ship, ship_start)
    lax.fori_loop(1, 3 * n_chunk, turn, 0)

    def dq_arrive(src, carry):
        @pl.when(half_dev * core + src != me)
        def _():
            pass
        return carry

    def arrive_dq(lo, hi):
        def body(src, carry):
            @pl.when((half_dev * core + src != me))
            def _():
                for k in range(2):
                    rcopy(dq_ref.at[pl.ds(0, rows), :],
                          dq_in.at[0, pl.ds(0, rows), pl.ds(0, wide)],
                          dq_send.at[0, k], dq_recv.at[src, k], sib).wait_recv()
            return carry
        lax.fori_loop(lo, hi, body, 0)

    def matmul(act, base, part):
        return lax.dot_general(act, w2[base + part], CONTRACT_LAST, preferred_element_type=F32)

    each(dq_ship, ship_wait)
    arrive_dq(0, half_dev)

    def first_pass(part, carry):
        acc[part] = matmul(dq_in[0], 0, part) + matmul(dq_in[1], n_chunk, part)
        return carry

    lax.fori_loop(0, n_chunk, first_pass, 0)

    each(dkv_ship, ship_wait)

    def dkv_arrive(src_chip, carry):
        @pl.when(src_chip != chip)
        def _():
            for k in range(2):
                rcopy(dkv_st.at[pl.ds(0, rows), :], dkv_in.at[pl.ds(0, rows), pl.ds(0, head)],
                      dkv_send.at[0, k], dkv_recv.at[src_chip, k], sib).wait_recv()
        return carry

    lax.fori_loop(0, n_chip, dkv_arrive, 0)

    sib_low = al((1 - core) * seg, seg)
    sib_high = al(rows + core * seg, seg)
    my_low = al(core * seg, seg)
    my_high = al(rows + (1 - core) * seg, seg)

    def far_copy(part, k):
        src_at = sib_low if k == 0 else sib_high
        return rcopy(acc.at[part, pl.ds(src_at, seg), :], far.at[part, pl.ds(k * seg, seg), :],
                     far_send.at[part, k], far_recv.at[part, k], sib)

    def last_pass(part, carry):
        acc[part] += matmul(dkv_in[...], 2 * n_chunk, part)

        @pl.when(part > 0)
        def _():
            for k in range(2):
                far_copy(part - 1, k).start()
        return carry

    lax.fori_loop(0, n_chunk, last_pass, 0)
    for k in range(2):
        far_copy(n_chunk - 1, k).start()

    def finish(part, carry):
        for k in range(2):
            far_copy(part, k).wait()
        lanes = pl.ds(al(part * D_CHUNK, D_CHUNK), D_CHUNK)
        dx_ref[pl.ds(0, seg), lanes] = (acc[part, pl.ds(my_low, seg), :] + far[part, pl.ds(0, seg), :]).astype(BF16)
        dx_ref[pl.ds(seg, seg), lanes] = (acc[part, pl.ds(my_high, seg), :] + far[part, pl.ds(seg, seg), :]).astype(BF16)
        return carry

    lax.fori_loop(0, n_chunk, finish, 0)


def solution(mesh):
    n_dev = mesh.shape["cp"]
    n_chip = n_dev // 2
    row_spec = P(("dp", "cp"), None)
    any_spec = pl.BlockSpec(memory_space=pl.ANY)
    vmem_spec = pl.BlockSpec(memory_space=pltpu.VMEM)
    dma = pltpu.SemaphoreType.DMA

    def device_fn(x_in, d_y, w_q, w_k, w_v, w_o):
        rows, d_model = x_in.shape
        q_heads, head = w_q.shape[1], w_q.shape[2]
        kv_heads = w_k.shape[1]
        seq = rows * n_dev
        scale = head ** -0.5
        wide = q_heads // n_dev * head
        tile_w = kv_heads * head
        n_chunk = d_model // D_CHUNK
        wo_flat = w_o.reshape(q_heads * head, d_model)
        params = functools.partial(pltpu.CompilerParams, vmem_limit_bytes=VMEM_LIMIT)
        q_all, do_all, kv_all = pl.pallas_call(
            functools.partial(project_kernel, n_dev),
            out_shape=(jax.ShapeDtypeStruct((seq, wide), BF16),
                       jax.ShapeDtypeStruct((seq, wide), BF16),
                       jax.ShapeDtypeStruct((2, seq, head), BF16)),
            in_specs=[vmem_spec, vmem_spec, any_spec, any_spec, any_spec, any_spec],
            out_specs=[any_spec] * 3,
            scratch_shapes=[
                pltpu.VMEM((2 * rows, d_model), BF16),
                pltpu.VMEM((2 * rows, d_model), BF16),
                pltpu.VMEM((WO_DEPTH, wide, d_model), BF16),
                pltpu.VMEM((DEPTH, D_CHUNK, kv_heads, head), BF16),
                pltpu.VMEM((2 * rows, tile_w), F32),
                pltpu.VMEM((n_chip, 2 * rows, wide), BF16),
                pltpu.VMEM((2 * rows, tile_w), BF16),
                pltpu.VMEM((2, 2 * rows, tile_w), BF16),
                dma((WO_DEPTH,)), dma((DEPTH,)), dma((2, 2)), dma((2, 2)),
                dma((n_chip, 2)), dma((n_chip, 2)), dma((n_chip, 2)), dma((n_chip, 2)),
                dma((n_chip, 2)), dma((n_chip, 2)), dma, dma,
            ],
            compiler_params=params(collective_id=0, has_side_effects=True),
            name="project",
        )(x_in, d_y, w_q, w_k, w_v, wo_flat)
        dq_all, dkv_part = pl.pallas_call(
            functools.partial(attend_kernel, scale),
            out_shape=(jax.ShapeDtypeStruct((seq, wide), BF16),
                       jax.ShapeDtypeStruct((2, seq, head), F32)),
            in_specs=[vmem_spec] * 3,
            out_specs=[vmem_spec] * 2,
            scratch_shapes=[
                pltpu.VMEM((head, seq), BF16),
                pltpu.VMEM((head, seq), BF16),
                pltpu.VMEM((wide // head, seq, 256), F32),
                pltpu.VMEM((wide // head, seq, 256), BF16),
            ],
            compiler_params=params(),
            name="attend",
        )(q_all, do_all, kv_all)
        return pl.pallas_call(
            functools.partial(collect_kernel, n_dev, scale),
            out_shape=jax.ShapeDtypeStruct((rows, d_model), BF16),
            in_specs=[vmem_spec, vmem_spec, any_spec, any_spec, any_spec],
            out_specs=vmem_spec,
            scratch_shapes=[
                pltpu.VMEM((2, 2 * rows, tile_w), BF16),
                pltpu.VMEM((2 * rows, tile_w), BF16),
                pltpu.VMEM((seq, head), F32),
                pltpu.VMEM((seq, head), BF16),
                pltpu.VMEM((DEPTH, D_CHUNK, kv_heads, head), BF16),
                pltpu.VMEM((3 * n_chunk, D_CHUNK, tile_w), BF16),
                pltpu.VMEM((n_chunk, 2 * rows, D_CHUNK), F32),
                pltpu.VMEM((n_chunk, rows, D_CHUNK), F32),
                dma((DEPTH,)), dma((n_chip, 2)), dma((n_chip, 2)), dma((n_chip, 2)), dma((n_chip, 2)),
                dma((n_chunk, 2)), dma((n_chunk, 2)), dma, dma,
            ],
            compiler_params=params(collective_id=1, has_side_effects=True),
            name="collect",
        )(dq_all, dkv_part, w_q, w_k, w_v)

    return jax.shard_map(device_fn, mesh=mesh, in_specs=(row_spec, row_spec, P(), P(), P(), P()),
                         out_specs=row_spec, check_vma=False)
```

time: 305 us -> 173 us (0.57); the launches traced: 300 us -> 173 us
  matrix products: 172 us -> 0 us
  Pallas kernels: 0 us -> 170 us
  waiting for transfers between devices: 80.6 us -> 0 us
  other arithmetic: 28.4 us -> 0 us
  between operations: 13.5 us -> 0.02 us
    dot_general x13 -> x0, matrix products: 172 us -> none  [the longest x1 24.4 us: device_fn(): jnp.einsum('bkrge,dkge->brd', dq_blocks, wq_grp, preferred_element_type=j...]
    pallas_call x0 -> x3, Pallas kernels: none -> 170 us  [the longest x1 78.2 us: device_fn(): pl.pallas_call(functools.partial(project_kernel, n_dev), out_shape=(jax.S...]
    reduce_scatter x2 -> x0, waiting for transfers between devices: 80.4 us -> none  [the longest x1 58.5 us: device_fn(): lax.psum_scatter(dv_part, 'cp', scatter_dimension=1, tiled=True)]
    reduce_sum x1 -> x0, other arithmetic: 16.6 us -> none  [block_step(): lse_blk = jax.nn.logsumexp(scores, axis=-1, keepdims=True)]
    convert_element_type x1 -> x0, other arithmetic: 9.46 us -> none  [block_step(): prob_blk = jnp.exp(scores - lse_blk).astype(jnp.bfloat16)]
  transfers between devices with their start and end apart: 4 -> 0, of which waited for: 2 -> 0; matrix products, arithmetic and copies ran while one was open for 48% -> 0% of each run, Pallas kernels for 0% -> 0%
where the time goes in v1:
time: 173 us
  Pallas kernels  170 us (98%)
  local copies, waits for them, and re-layouts  2.46 us (1%)
    pallas_call x1, Pallas kernels, device_fn(): pl.pallas_call(functools.partial(project_kernel, n_dev), out_shape=(jax.S...  78.2 us
    pallas_call x1, Pallas kernels, device_fn(): pl.pallas_call(functools.partial(collect_kernel, n_dev, scale), out_shape...  50.8 us
    pallas_call x1, Pallas kernels, device_fn(): pl.pallas_call(functools.partial(attend_kernel, scale), out_shape=(jax.Sh...  41.2 us

profile of v1, /device:TPU:21, one launch (start us, length us, event | category | flops | bytes accessed | tf_op | source)
XLA Modules:
  0.0 172.6 jit_solution(15792256050781399016)
XLA Ops:
  0.0 78.2 %project.1 = (bf16[2048,256]{1,0:T(8,128)(2,1)}, bf16[2048,256]{1,0:T(8,128)(2,1)}, bf16[2,2048,128]{2,1,0:T(8,128)(2,1)}) custom-call(bf16[128,5120]{1,0:T(8,128)(2,1)} %x_ref.1, bf16[128,5120]{1,0:T(8,128)(2,1)} %dy_ref.1, bf16[5120,32,128]{2,1,0:T(8,128)(2,1)} %wq.3, bf16[5120,8,128]{2,1,0:T(8,128)(2,1)} %wk.3, bf16[5120,8,128]{2,1,0:T(8,128)(2,1)} %wv.3, ...), custom_call_target="tpu_custom_call" | custom-call | tf_op jit(solution)/shard_map/project/pallas_call | solution.py:526
  78.2 41.2 %attend.1 = (bf16[2048,256]{1,0:T(8,128)(2,1)}, f32[2,2048,128]{2,1,0:T(8,128)}) custom-call(bf16[2048,256]{1,0:T(8,128)(2,1)} %get-tuple-element.10.q_ref, bf16[2048,256]{1,0:T(8,128)(2,1)} %get-tuple-element.11.do_ref, bf16[2,2048,128]{2,1,0:T(8,128)(2,1)} %get-tuple-element.12.kv_ref), custom_call_target="tpu_custom_call" | custom-call | tf_op jit(solution)/shard_map/attend/pallas_call | solution.py:549
  119.3 50.8 %collect.1 = bf16[128,5120]{1,0:T(8,128)(2,1)} custom-call(bf16[2048,256]{1,0:T(8,128)(2,1)} %get-tuple-element.13.dq_ref, f32[2,2048,128]{2,1,0:T(8,128)} %get-tuple-element.14.dkv_ref, bf16[5120,32,128]{2,1,0:T(8,128)(2,1)} %wq.3, bf16[5120,8,128]{2,1,0:T(8,128)(2,1)} %wk.3, bf16[5120,8,128]{2,1,0:T(8,128)(2,1)} %wv.3), custom_call_target="tpu_custom_call" | custom-call | tf_op jit(solution)/shard_map/collect/pallas_call | solution.py:564
  170.1 2.5 %copy.8 = bf16[128,5120]{1,0:T(8,128)(2,1)} copy(bf16[128,5120]{1,0:T(8,128)(2,1)} %collect.1) | data formatting | bytes 2621440

commit v2 on v1

--- a/solution.py
+++ b/solution.py
@@ -14,6 +14,8 @@
 DEPTH = 4
 WO_DEPTH = 3
 D_CHUNK = 512
+BQ = 256
+BK = 512
 VMEM_LIMIT = 62 * 2 ** 20
 
 
@@ -67,9 +69,9 @@
         rcopy(src, dst, send_sem, recv_sem, dev).wait_send()
 
 
-def project_kernel(n_dev, x_ref, dy_ref, wq, wk, wv, wo, q_all, do_all, kv_all,
-                   xs, dys, wo_buf, w_buf, acc, st_do, st_kv, st_q,
-                   wo_sem, w_sem, x_send, x_recv, do_send, do_recv,
+def project_kernel(n_dev, x_ref, dy_ref, wq, wk, wv, wo, q_all, do_all, kv_all, w2_all,
+                   xs, dys, wo_buf, w_buf, w2_buf, acc, st_do, st_kv, st_q,
+                   wo_sem, w_sem, w2_sem, x_send, x_recv, do_send, do_recv,
                    kv_send, kv_recv, q_send, q_recv, rel_send, rel_recv):
     me, chip, core, sib = place()
     n_chip = n_dev // 2
@@ -165,11 +167,27 @@
     swaps[2].wait()
     swaps[3].wait()
 
+    def w2_copy(s):
+        part = lax.rem(s, n_chunk)
+        kind = s // n_chunk
+        group = jnp.where(kind == 0, 0, 1 + lax.rem(kind - 1 + chip // 2, 2))
+        slot = lax.rem(s, DEPTH)
+        return pltpu.make_async_copy(w2_buf.at[slot], w2_all.at[group * n_chunk + part], w2_sem.at[slot])
+
     def w_step(s, first):
         w_start(s + DEPTH - 1)
         w_wait(s)
+
+        @pl.when(s >= 1)
+        def _():
+            w2_copy(s - 1).start()
+
+        @pl.when(s >= DEPTH)
+        def _():
+            w2_copy(s - DEPTH).wait()
         part = lax.rem(s, n_chunk)
         w_tile = w_buf[lax.rem(s, DEPTH)].reshape(D_CHUNK, tile_w)
+        w2_buf[lax.rem(s, DEPTH)] = w_tile
         add = jnp.dot(xs[:, pl.ds(al(part * D_CHUNK, D_CHUNK), D_CHUNK)], w_tile,
                       preferred_element_type=F32)
         acc[...] = add if first else acc[...] + add
@@ -206,15 +224,15 @@
             return carry
         lax.fori_loop(0, 4, body, 0)
 
-    w_step(0, True)
+    w_step(jnp.int32(0), True)
     do_ship(n_dest - 1, ship_start)
     w_loop(1, n_chunk)
     st_kv[...] = acc[...].astype(BF16)
-    w_step(n_chunk, True)
+    w_step(jnp.int32(n_chunk), True)
     kv_ship_all(ship_start)
     w_loop(n_chunk + 1, 2 * n_chunk)
     st_q[0] = acc[...].astype(BF16)
-    w_step(2 * n_chunk, True)
+    w_step(jnp.int32(2 * n_chunk), True)
     q_ship_all(0, ship_start)
     w_loop(2 * n_chunk + 1, 3 * n_chunk)
     st_q[1] = acc[...].astype(BF16)
@@ -229,6 +247,9 @@
 
     lax.fori_loop(0, n_chip, kv_arrive, 0)
     q_ship_all(1, ship_start)
+    w2_copy(jnp.int32(3 * n_chunk - 1)).start()
+    for k in range(DEPTH):
+        w2_copy(jnp.int32(3 * n_chunk - DEPTH + k)).wait()
     kv_ship_all(ship_wait)
     relay = rcopy(kv_all.at[core], kv_all.at[core], rel_send, rel_recv, sib)
     relay.start()
@@ -256,209 +277,163 @@
     relay.wait_send()
 
 
-def attend_kernel(scale, q_ref, do_ref, kv_ref, dq_ref, dkv_ref, k_t, v_t, s_scr, p_scr):
+def attend_kernel(n_dev, scale, q_ref, do_ref, kv_ref, w2_hbm, dx_ref,
+                  k_t, v_t, s_scr, p_scr, dq_st, dkv_acc, dq_in, dkv_in, dkv_far, dkv_st, w2, acc, far,
+                  w_sem, dq_send, dq_recv, dkv_send, dkv_recv, far_send, far_recv, red_send, red_recv):
+    me, chip, core, sib = place()
+    n_chip = n_dev // 2
+    rows, d_model = dx_ref.shape
+    seg = rows // 2
     seq, wide = q_ref.shape
     head = kv_ref.shape[2]
     heads = wide // head
-    bq, bk = 256, 512
+    n_chunk = d_model // D_CHUNK
+    half_dev = n_dev // 2
+    dq_core = chip // (n_chip // 2)
+    src_slot = lax.rem(me, half_dev)
+    n_block = seq // BQ
+    to_log2 = scale * 1.4426950408889634
+
+    def w2_copy(group):
+        part = pl.ds(group * n_chunk, n_chunk)
+        return pltpu.make_async_copy(w2_hbm.at[part], w2.at[part], w_sem.at[group])
+
+    for group in range(3):
+        w2_copy(group).start()
+    barrier = pltpu.get_barrier_semaphore()
+
+    def greet(step, carry):
+        other = lax.rem(me + step, n_dev)
+        pl.semaphore_signal(barrier, inc=1, device_id={"cp": other}, device_id_type=MESH)
+        return carry
+
+    lax.fori_loop(1, n_dev, greet, 0)
     k_t[...] = kv_ref[0].T
     v_t[...] = kv_ref[1].T
-    dkv_ref[...] = jnp.zeros_like(dkv_ref)
-    to_log2 = scale * 1.4426950408889634
-
-    def q_block(qb, carry):
-        q_rows = pl.ds(al(qb * bq, bq), bq)
+    dkv_acc[...] = jnp.zeros_like(dkv_acc)
+
+    def body(qb):
+        q_rows = slice(qb * BQ, (qb + 1) * BQ)
         q = [q_ref[q_rows, h * head:(h + 1) * head] for h in range(heads)]
         do = [do_ref[q_rows, h * head:(h + 1) * head] for h in range(heads)]
-        last = (qb * bq) // bk
-
-        def keys(kc):
-            return pl.ds(al(kc * bk, bk), bk)
-
-        def scores(kc, tops, masked):
-            k_blk = kv_ref[0, keys(kc), :]
-            out = []
+        cuts = list(range(0, qb * BQ, BK)) + [qb * BQ, (qb + 1) * BQ]
+        chunks = [slice(lo, hi) for lo, hi in zip(cuts[:-1], cuts[1:])]
+        tops = [[] for _ in range(heads)]
+        sums = [[] for _ in range(heads)]
+        for ks in chunks:
+            k_blk = kv_ref[0, ks, :]
             for h in range(heads):
                 s = lax.dot_general(k_blk, q[h], CONTRACT_LAST, preferred_element_type=F32)
-                if masked:
-                    k_pos = kc * bk + lax.broadcasted_iota(jnp.int32, (bk, bq), 0)
-                    q_pos = qb * bq + lax.broadcasted_iota(jnp.int32, (bk, bq), 1)
+                if ks.start == qb * BQ:
+                    k_pos = lax.broadcasted_iota(jnp.int32, (BQ, BQ), 0)
+                    q_pos = lax.broadcasted_iota(jnp.int32, (BQ, BQ), 1)
                     s = jnp.where(k_pos <= q_pos, s, -jnp.inf)
-                s_scr[h, keys(kc), :] = s
-                out.append(jnp.maximum(tops[h], jnp.max(s, axis=0, keepdims=True)))
-            return tuple(out)
-
-        tops = tuple(jnp.full((1, bq), -jnp.inf, F32) for _ in range(heads))
-        tops = lax.fori_loop(0, last, lambda kc, c: scores(kc, c, False), tops)
-        tops = scores(last, tops, True)
-        tops = [t * to_log2 for t in tops]
-
-        def expo(kc, sums):
-            out = []
-            for h in range(heads):
-                e = jnp.exp2(s_scr[h, keys(kc), :] * to_log2 - tops[h])
-                s_scr[h, keys(kc), :] = e
-                out.append(sums[h] + jnp.sum(e, axis=0, keepdims=True))
-            return tuple(out)
-
-        sums = lax.fori_loop(0, last + 1, expo, tuple(jnp.zeros((1, bq), F32) for _ in range(heads)))
-        inv = [1.0 / s for s in sums]
-
-        def outs(kc, acc):
-            v_blk = v_t[:, keys(kc)]
-            out = []
-            for h in range(heads):
-                p = (s_scr[h, keys(kc), :] * inv[h]).astype(BF16)
-                p_scr[h, keys(kc), :] = p
-                out.append(acc[h] + jnp.dot(v_blk, p, preferred_element_type=F32))
-            return tuple(out)
-
-        zero = tuple(jnp.zeros((head, bq), F32) for _ in range(heads))
-        o_t = lax.fori_loop(0, last + 1, outs, zero)
-        delta = [jnp.sum(do[h].astype(F32).T * o_t[h].astype(BF16).astype(F32), axis=0, keepdims=True)
-                 for h in range(heads)]
-
-        def grads(kc, acc):
-            k_blk = k_t[:, keys(kc)]
-            v_blk = kv_ref[1, keys(kc), :]
-            out = []
+                top = jnp.max(s, axis=0, keepdims=True) * to_log2
+                e = jnp.exp2(s * to_log2 - top)
+                s_scr[h, ks, :] = e
+                tops[h].append(top)
+                sums[h].append(jnp.sum(e, axis=0, keepdims=True))
+        delta = []
+        for h in range(heads):
+            top = functools.reduce(jnp.maximum, tops[h])
+            lift = [jnp.exp2(t - top) for t in tops[h]]
+            inv = 1.0 / sum(a * b for a, b in zip(lift, sums[h]))
+            o_t = None
+            for ks, up in zip(chunks, lift):
+                p = (s_scr[h, ks, :] * (up * inv)).astype(BF16)
+                p_scr[h, ks, :] = p
+                part = jnp.dot(v_t[:, ks], p, preferred_element_type=F32)
+                o_t = part if o_t is None else o_t + part
+            delta.append(jnp.sum(do[h].astype(F32).T * o_t.astype(BF16).astype(F32), axis=0, keepdims=True))
+        dq_t = [None] * heads
+        for ks in chunks:
+            v_blk = kv_ref[1, ks, :]
             dk = dv = None
             for h in range(heads):
-                p = p_scr[h, keys(kc), :]
+                p = p_scr[h, ks, :]
                 dp = lax.dot_general(v_blk, do[h], CONTRACT_LAST, preferred_element_type=F32)
                 ds = (p.astype(F32) * (dp - delta[h])).astype(BF16)
-                out.append(acc[h] + jnp.dot(k_blk, ds, preferred_element_type=F32))
+                part = jnp.dot(k_t[:, ks], ds, preferred_element_type=F32)
+                dq_t[h] = part if dq_t[h] is None else dq_t[h] + part
                 dk_h = jnp.dot(ds, q[h], preferred_element_type=F32)
                 dv_h = jnp.dot(p, do[h], preferred_element_type=F32)
                 dk = dk_h if dk is None else dk + dk_h
                 dv = dv_h if dv is None else dv + dv_h
-            dkv_ref[0, keys(kc), :] += dk
-            dkv_ref[1, keys(kc), :] += dv
-            return tuple(out)
-
-        dq_t = lax.fori_loop(0, last + 1, grads, zero)
+            dkv_acc[0, ks, :] += dk
+            dkv_acc[1, ks, :] += dv
         for h in range(heads):
-            dq_ref[q_rows, h * head:(h + 1) * head] = (dq_t[h] * scale).T.astype(BF16)
-        return carry
-
-    lax.fori_loop(0, seq // bq, q_block, 0)
-
-
-def collect_kernel(n_dev, scale, dq_ref, dkv_ref, wq, wk, wv, dx_ref,
-                   dq_in, dkv_in, dkv_far, dkv_st, w_buf, w2, acc, far,
-                   w_sem, dq_send, dq_recv, dkv_send, dkv_recv, far_send, far_recv, red_send, red_recv):
-    me, chip, core, sib = place()
-    n_chip = n_dev // 2
-    rows, d_model = dx_ref.shape
-    seg = rows // 2
-    head = dkv_ref.shape[2]
-    wide = dq_ref.shape[1]
-    n_chunk = d_model // D_CHUNK
-    tile_heads = w_buf.shape[2]
-    tile_w = w2.shape[2]
-    half_dev = n_dev // 2
-    dq_core = chip // (n_chip // 2)
-
-    def w_start(s):
-        slot = lax.rem(s, DEPTH)
-        part = lax.rem(s, n_chunk)
-        d_rows = pl.ds(al(part * D_CHUNK, D_CHUNK), D_CHUNK)
-
-        @pl.when(s < 2 * n_chunk)
-        def _():
-            tile = 2 * core + s // n_chunk
-            pltpu.make_async_copy(
-                wq.at[d_rows, pl.ds(al(tile * tile_heads, tile_heads), tile_heads), :],
-                w_buf.at[slot], w_sem.at[slot]).start()
-
-        @pl.when((s >= 2 * n_chunk) & (s < 3 * n_chunk) & (core == 0))
-        def _():
-            pltpu.make_async_copy(wk.at[d_rows], w_buf.at[slot], w_sem.at[slot]).start()
-
-        @pl.when((s >= 2 * n_chunk) & (s < 3 * n_chunk) & (core == 1))
-        def _():
-            pltpu.make_async_copy(wv.at[d_rows], w_buf.at[slot], w_sem.at[slot]).start()
-
-    for s in range(DEPTH - 1):
-        w_start(s)
-    meet_group(n_dev)
-    swap = rcopy(dkv_ref.at[1 - core], dkv_far, red_send, red_recv, sib)
+            dq_st[q_rows, h * head:(h + 1) * head] = (dq_t[h] * scale).T.astype(BF16)
+
+    def dq_ship(block, act):
+        k = block // n_chip
+        dest_chip = jnp.where(k == 0, block, 2 * n_chip - 1 - block)
+        dest = 2 * dest_chip + dq_core
+        act(dest == me, dq_st.at[pl.ds(al(block * rows, rows), rows), :],
+            dq_in.at[src_slot // 4, pl.ds(al(k * rows, rows), rows), pl.ds(al(lax.rem(src_slot, 4) * wide, wide), wide)],
+            dq_send.at[block], dq_recv.at[src_slot, k], dest)
+
+    per = BQ // rows
+
+    def turn(step, carry):
+        qb = lax.rem(chip + step, n_block)
+        for which in range(n_block):
+            @pl.when(qb == which)
+            def _():
+                body(which)
+
+        @pl.when(step == 0)
+        def _():
+            pl.semaphore_wait(barrier, n_dev - 1)
+        for i in range(per):
+            dq_ship(qb * per + i, ship_start)
+        return carry
+
+    lax.fori_loop(0, n_block, turn, 0)
+    swap = rcopy(dkv_acc.at[1 - core], dkv_far, red_send, red_recv, sib)
     swap.start()
-
-    src_slot = lax.rem(me, half_dev)
-
-    def at_of(dest_chip, k):
-        block = dest_chip if k == 0 else 2 * n_chip - 1 - dest_chip
-        return al(block * rows, rows)
-
-    def dq_ship(n, act):
-        dest_chip = lax.rem(chip + n, n_chip)
-        dest = 2 * dest_chip + dq_core
-        for k in range(2):
-            act(dest == me, dq_ref.at[pl.ds(at_of(dest_chip, k), rows), :],
-                dq_in.at[src_slot // 4, pl.ds(k * rows, rows), pl.ds(al(lax.rem(src_slot, 4) * wide, wide), wide)],
-                dq_send.at[n, k], dq_recv.at[src_slot, k], dest)
 
     def dkv_ship(n, act):
         dest_chip = lax.rem(chip + n, n_chip)
         dest = 2 * dest_chip + core
         for k in range(2):
-            act(dest == me, dkv_st.at[pl.ds(at_of(dest_chip, k), rows), :],
+            block = dest_chip if k == 0 else 2 * n_chip - 1 - dest_chip
+            act(dest == me, dkv_st.at[pl.ds(al(block * rows, rows), rows), :],
                 dkv_in.at[pl.ds(k * rows, rows), pl.ds(al(chip * head, head), head)],
                 dkv_send.at[n, k], dkv_recv.at[chip, k], dest)
 
-    def each(ship, act):
-        def body(n, carry):
+    def each(count, ship, act):
+        def step(n, carry):
             ship(n, act)
             return carry
-        lax.fori_loop(0, n_chip, body, 0)
-
-    each(dq_ship, ship_start)
+        lax.fori_loop(0, count, step, 0)
+
     swap.wait()
     factor = jnp.where(core == 0, scale, 1.0).astype(F32)
-    dkv_st[...] = ((dkv_ref[core] + dkv_far[...]) * factor).astype(BF16)
-
-    def turn(s, carry):
-        w_start(s + DEPTH - 1)
-        slot = lax.rem(s, DEPTH)
-        pltpu.make_async_copy(wk.at[pl.ds(0, D_CHUNK)], w_buf.at[slot], w_sem.at[slot]).wait()
-        w2[s] = w_buf[slot].reshape(D_CHUNK, tile_w)
-        return carry
-
-    turn(0, 0)
-    each(dkv_ship, ship_start)
-    lax.fori_loop(1, 3 * n_chunk, turn, 0)
+    dkv_st[...] = ((dkv_acc[core] + dkv_far[...]) * factor).astype(BF16)
+    for group in range(3):
+        w2_copy(group).wait()
+    each(n_chip, dkv_ship, ship_start)
 
     def dq_arrive(src, carry):
         @pl.when(half_dev * core + src != me)
         def _():
-            pass
-        return carry
-
-    def arrive_dq(lo, hi):
-        def body(src, carry):
-            @pl.when((half_dev * core + src != me))
-            def _():
-                for k in range(2):
-                    rcopy(dq_ref.at[pl.ds(0, rows), :],
-                          dq_in.at[0, pl.ds(0, rows), pl.ds(0, wide)],
-                          dq_send.at[0, k], dq_recv.at[src, k], sib).wait_recv()
-            return carry
-        lax.fori_loop(lo, hi, body, 0)
+            for k in range(2):
+                rcopy(dq_st.at[pl.ds(0, rows), :], dq_in.at[0, pl.ds(0, rows), pl.ds(0, wide)],
+                      dq_send.at[0], dq_recv.at[src, k], sib).wait_recv()
+        return carry
 
     def matmul(act, base, part):
         return lax.dot_general(act, w2[base + part], CONTRACT_LAST, preferred_element_type=F32)
 
-    each(dq_ship, ship_wait)
-    arrive_dq(0, half_dev)
+    each(n_block * per, dq_ship, ship_wait)
+    lax.fori_loop(0, half_dev, dq_arrive, 0)
 
     def first_pass(part, carry):
-        acc[part] = matmul(dq_in[0], 0, part) + matmul(dq_in[1], n_chunk, part)
+        acc[part] = matmul(dq_in[0], n_chunk, part) + matmul(dq_in[1], 2 * n_chunk, part)
         return carry
 
     lax.fori_loop(0, n_chunk, first_pass, 0)
-
-    each(dkv_ship, ship_wait)
+    each(n_chip, dkv_ship, ship_wait)
 
     def dkv_arrive(src_chip, carry):
         @pl.when(src_chip != chip)
@@ -481,7 +456,7 @@
                      far_send.at[part, k], far_recv.at[part, k], sib)
 
     def last_pass(part, carry):
-        acc[part] += matmul(dkv_in[...], 2 * n_chunk, part)
+        acc[part] += matmul(dkv_in[...], 0, part)
 
         @pl.when(part > 0)
         def _():
@@ -523,64 +498,56 @@
         n_chunk = d_model // D_CHUNK
         wo_flat = w_o.reshape(q_heads * head, d_model)
         params = functools.partial(pltpu.CompilerParams, vmem_limit_bytes=VMEM_LIMIT)
-        q_all, do_all, kv_all = pl.pallas_call(
+        q_all, do_all, kv_all, w2_all = pl.pallas_call(
             functools.partial(project_kernel, n_dev),
             out_shape=(jax.ShapeDtypeStruct((seq, wide), BF16),
                        jax.ShapeDtypeStruct((seq, wide), BF16),
-                       jax.ShapeDtypeStruct((2, seq, head), BF16)),
+                       jax.ShapeDtypeStruct((2, seq, head), BF16),
+                       jax.ShapeDtypeStruct((3 * n_chunk, D_CHUNK, tile_w), BF16)),
             in_specs=[vmem_spec, vmem_spec, any_spec, any_spec, any_spec, any_spec],
-            out_specs=[any_spec] * 3,
+            out_specs=[any_spec] * 4,
             scratch_shapes=[
                 pltpu.VMEM((2 * rows, d_model), BF16),
                 pltpu.VMEM((2 * rows, d_model), BF16),
                 pltpu.VMEM((WO_DEPTH, wide, d_model), BF16),
                 pltpu.VMEM((DEPTH, D_CHUNK, kv_heads, head), BF16),
+                pltpu.VMEM((DEPTH, D_CHUNK, tile_w), BF16),
                 pltpu.VMEM((2 * rows, tile_w), F32),
                 pltpu.VMEM((n_chip, 2 * rows, wide), BF16),
                 pltpu.VMEM((2 * rows, tile_w), BF16),
                 pltpu.VMEM((2, 2 * rows, tile_w), BF16),
-                dma((WO_DEPTH,)), dma((DEPTH,)), dma((2, 2)), dma((2, 2)),
+                dma((WO_DEPTH,)), dma((DEPTH,)), dma((DEPTH,)), dma((2, 2)), dma((2, 2)),
                 dma((n_chip, 2)), dma((n_chip, 2)), dma((n_chip, 2)), dma((n_chip, 2)),
                 dma((n_chip, 2)), dma((n_chip, 2)), dma, dma,
             ],
             compiler_params=params(collective_id=0, has_side_effects=True),
             name="project",
         )(x_in, d_y, w_q, w_k, w_v, wo_flat)
-        dq_all, dkv_part = pl.pallas_call(
-            functools.partial(attend_kernel, scale),
-            out_shape=(jax.ShapeDtypeStruct((seq, wide), BF16),
-                       jax.ShapeDtypeStruct((2, seq, head), F32)),
-            in_specs=[vmem_spec] * 3,
-            out_specs=[vmem_spec] * 2,
+        return pl.pallas_call(
+            functools.partial(attend_kernel, n_dev, scale),
+            out_shape=jax.ShapeDtypeStruct((rows, d_model), BF16),
+            in_specs=[vmem_spec, vmem_spec, vmem_spec, any_spec],
+            out_specs=vmem_spec,
             scratch_shapes=[
                 pltpu.VMEM((head, seq), BF16),
                 pltpu.VMEM((head, seq), BF16),
-                pltpu.VMEM((wide // head, seq, 256), F32),
-                pltpu.VMEM((wide // head, seq, 256), BF16),
-            ],
-            compiler_params=params(),
-            name="attend",
-        )(q_all, do_all, kv_all)
-        return pl.pallas_call(
-            functools.partial(collect_kernel, n_dev, scale),
-            out_shape=jax.ShapeDtypeStruct((rows, d_model), BF16),
-            in_specs=[vmem_spec, vmem_spec, any_spec, any_spec, any_spec],
-            out_specs=vmem_spec,
-            scratch_shapes=[
+                pltpu.VMEM((wide // head, seq, BQ), F32),
+                pltpu.VMEM((wide // head, seq, BQ), BF16),
+                pltpu.VMEM((seq, wide), BF16),
+                pltpu.VMEM((2, seq, head), F32),
                 pltpu.VMEM((2, 2 * rows, tile_w), BF16),
                 pltpu.VMEM((2 * rows, tile_w), BF16),
                 pltpu.VMEM((seq, head), F32),
                 pltpu.VMEM((seq, head), BF16),
-                pltpu.VMEM((DEPTH, D_CHUNK, kv_heads, head), BF16),
                 pltpu.VMEM((3 * n_chunk, D_CHUNK, tile_w), BF16),
                 pltpu.VMEM((n_chunk, 2 * rows, D_CHUNK), F32),
                 pltpu.VMEM((n_chunk, rows, D_CHUNK), F32),
-                dma((DEPTH,)), dma((n_chip, 2)), dma((n_chip, 2)), dma((n_chip, 2)), dma((n_chip, 2)),
+                dma((3,)), dma((seq // rows,)), dma((n_chip, 2)), dma((n_chip, 2)), dma((n_chip, 2)),
                 dma((n_chunk, 2)), dma((n_chunk, 2)), dma, dma,
             ],
             compiler_params=params(collective_id=1, has_side_effects=True),
-            name="collect",
-        )(dq_all, dkv_part, w_q, w_k, w_v)
+            name="attend",
+        )(q_all, do_all, kv_all, w2_all)
 
     return jax.shard_map(device_fn, mesh=mesh, in_specs=(row_spec, row_spec, P(), P(), P(), P()),
                          out_specs=row_spec, check_vma=False)

time: 173 us -> 140 us (0.81)
  Pallas kernels: 170 us -> 137 us
    pallas_call x2 -> x1, Pallas kernels: 91.9 us -> 59.2 us  [device_fn(): pl.pallas_call(functools.partial(attend_kernel, n_dev, scale), out_shape=...]
where the time goes in v2:
time: 140 us; the launch traced here: 139 us
  Pallas kernels  137 us (98%)
  local copies, waits for them, and re-layouts  2.46 us (2%)
    pallas_call x1, Pallas kernels, device_fn(): pl.pallas_call(functools.partial(project_kernel, n_dev), out_shape=(jax.S...  77.8 us
    pallas_call x1, Pallas kernels, device_fn(): pl.pallas_call(functools.partial(attend_kernel, n_dev, scale), out_shape=...  59.2 us

profile of v2, /device:TPU:21, one launch (start us, length us, event | category | flops | bytes accessed | tf_op | source)
XLA Modules:
  0.0 139.5 jit_solution(4588530546739869282)
XLA Ops:
  0.0 77.8 %project.1 = (bf16[2048,256]{1,0:T(8,128)(2,1)}, bf16[2048,256]{1,0:T(8,128)(2,1)}, bf16[2,2048,128]{2,1,0:T(8,128)(2,1)}, bf16[30,512,1024]{2,1,0:T(8,128)(2,1)}) custom-call(bf16[128,5120]{1,0:T(8,128)(2,1)} %x_ref.1, bf16[128,5120]{1,0:T(8,128)(2,1)} %dy_ref.1, bf16[5120,32,128]{2,1,0:T(8,128)(2,1)} %wq.1, bf16[5120,8,128]{2,1,0:T(8,128)(2,1)} %wk.1, ...), custom_call_target="tpu_custom_call" | custom-call | tf_op jit(solution)/shard_map/project/pallas_call | solution.py:501
  77.8 59.2 %attend.1 = bf16[128,5120]{1,0:T(8,128)(2,1)} custom-call(bf16[2048,256]{1,0:T(8,128)(2,1)} %get-tuple-element.9.q_ref, bf16[2048,256]{1,0:T(8,128)(2,1)} %get-tuple-element.10.do_ref, bf16[2,2048,128]{2,1,0:T(8,128)(2,1)} %get-tuple-element.11.kv_ref, bf16[30,512,1024]{2,1,0:T(8,128)(2,1)} %get-tuple-element.12.w2_hbm), custom_call_target="tpu_custom_call" | custom-call | tf_op jit(solution)/shard_map/attend/pallas_call | solution.py:526
  137.0 2.5 %copy.8 = bf16[128,5120]{1,0:T(8,128)(2,1)} copy(bf16[128,5120]{1,0:T(8,128)(2,1)} %attend.1) | data formatting | bytes 2621440

commit v3 on v2

v3 whole, which is shorter than its diff:
```python
import functools

import jax
import jax.numpy as jnp
from jax import lax
from jax.experimental import pallas as pl
from jax.experimental.pallas import tpu as pltpu
from jax.sharding import PartitionSpec as P

MESH = pl.DeviceIdType.MESH
BF16 = jnp.bfloat16
F32 = jnp.float32
CONTRACT_LAST = (((1,), (1,)), ((), ()))
DEPTH = 4
WO_DEPTH = 2
D_CHUNK = 512
BQ = 256
BK = 512
DO_FIRST = 2
VMEM_LIMIT = 62 * 2 ** 20


def place():
    me = lax.axis_index("cp")
    chip = me // 2
    core = me % 2
    return me, chip, core, me + 1 - 2 * core


def meet_group(n_dev):
    me = lax.axis_index("cp")
    barrier = pltpu.get_barrier_semaphore()

    def greet(step, carry):
        other = lax.rem(me + step, n_dev)
        pl.semaphore_signal(barrier, inc=1, device_id={"cp": other}, device_id_type=MESH)
        return carry

    lax.fori_loop(1, n_dev, greet, 0)
    pl.semaphore_wait(barrier, n_dev - 1)


def rcopy(src, dst, send_sem, recv_sem, dev):
    return pltpu.make_async_remote_copy(
        src_ref=src, dst_ref=dst, send_sem=send_sem, recv_sem=recv_sem,
        device_id={"cp": dev}, device_id_type=MESH)


def al(value, step):
    return pl.multiple_of(value, step)


def ship_start(is_me, src, dst, send_sem, recv_sem, dev):
    @pl.when(is_me)
    def _():
        pltpu.make_async_copy(src, dst, send_sem).start()

    @pl.when(jnp.logical_not(is_me))
    def _():
        rcopy(src, dst, send_sem, recv_sem, dev).start()


def ship_wait(is_me, src, dst, send_sem, recv_sem, dev):
    @pl.when(is_me)
    def _():
        pltpu.make_async_copy(src, dst, send_sem).wait()

    @pl.when(jnp.logical_not(is_me))
    def _():
        rcopy(src, dst, send_sem, recv_sem, dev).wait_send()


def fused_kernel(n_dev, scale, x_ref, dy_ref, wq, wk, wv, wo, dx_ref, w2_all,
                 xs, dys, wo_buf, w_buf, w2_buf, p_acc, st_do, st_kv, st_q,
                 q_all, do_all, kv_all, k_t, v_t, p_all, o_all, dq_st, dkv_acc,
                 dq_in, dkv_in, dkv_far, dkv_st, acc, far,
                 wo_sem, w_sem, w2_sem, x_send, x_recv, do_send, do_recv,
                 kv_send, kv_recv, q_send, q_recv, rel_send, rel_recv,
                 dq_send, dq_recv, dkv_send, dkv_recv, far_send, far_recv, red_send, red_recv):
    me, chip, core, sib = place()
    n_chip = n_dev // 2
    rows, d_model = x_ref.shape
    seg = rows // 2
    seq, wide = q_all.shape
    head = kv_all.shape[2]
    heads = wide // head
    tile_w = p_acc.shape[1]
    n_chunk = d_model // D_CHUNK
    n_dest = n_dev // 2
    tile_heads = w_buf.shape[2]
    my_src_core = chip // (n_chip // 2)
    low_at = al(chip * rows, rows)
    high_at = al((2 * n_chip - 1 - chip) * rows, rows)
    n_block = seq // BQ
    per = BQ // rows
    to_log2 = scale * 1.4426950408889634

    def dest_of(n):
        return n_dest * core + lax.rem(2 * n_chip + 2 * chip - 2 * (n // 2) + lax.rem(n, 2), n_dest)

    def wo_copy(n):
        return pltpu.make_async_copy(
            wo.at[pl.ds(al(dest_of(n) * wide, wide), wide), :], wo_buf.at[lax.rem(n, WO_DEPTH)],
            wo_sem.at[lax.rem(n, WO_DEPTH)])

    def tile_of(t):
        return 2 * core + lax.rem(t + chip // 2, 2)

    def w_start(s):
        slot = lax.rem(s, DEPTH)
        part = lax.rem(s, n_chunk)
        d_rows = pl.ds(al(part * D_CHUNK, D_CHUNK), D_CHUNK)

        @pl.when((s < n_chunk) & (core == 0))
        def _():
            pltpu.make_async_copy(wk.at[d_rows], w_buf.at[slot], w_sem.at[slot]).start()

        @pl.when((s < n_chunk) & (core == 1))
        def _():
            pltpu.make_async_copy(wv.at[d_rows], w_buf.at[slot], w_sem.at[slot]).start()

        @pl.when((s >= n_chunk) & (s < 3 * n_chunk))
        def _():
            tile = tile_of(s // n_chunk - 1)
            pltpu.make_async_copy(
                wq.at[d_rows, pl.ds(al(tile * tile_heads, tile_heads), tile_heads), :],
                w_buf.at[slot], w_sem.at[slot]).start()

    def w_wait(s):
        slot = lax.rem(s, DEPTH)
        pltpu.make_async_copy(wk.at[pl.ds(0, D_CHUNK)], w_buf.at[slot], w_sem.at[slot]).wait()

    for n in range(WO_DEPTH - 1):
        wo_copy(jnp.int32(n)).start()
    for s in range(DEPTH - 1):
        w_start(jnp.int32(s))

    my_low = al(core * seg, seg)
    my_high = al(rows + (1 - core) * seg, seg)
    for ref, stack in ((dy_ref, dys), (x_ref, xs)):
        stack[pl.ds(my_low, seg), :] = ref[:seg, :]
        stack[pl.ds(my_high, seg), :] = ref[seg:, :]
    dkv_acc[...] = jnp.zeros_like(dkv_acc)
    meet_group(n_dev)
    swaps = []
    for k, (ref, stack) in enumerate(((dy_ref, dys), (x_ref, xs))):
        swaps.append(rcopy(ref.at[pl.ds(0, seg)], stack.at[pl.ds(my_low, seg)],
                           x_send.at[k, 0], x_recv.at[k, 0], sib))
        swaps.append(rcopy(ref.at[pl.ds(seg, seg)], stack.at[pl.ds(my_high, seg)],
                           x_send.at[k, 1], x_recv.at[k, 1], sib))
    for swap in swaps:
        swap.start()
    swaps[0].wait()
    swaps[1].wait()

    def each(lo, hi, ship, act):
        def step(n, carry):
            ship(n, act)
            return carry
        lax.fori_loop(lo, hi, step, 0)

    def do_ship(n, act):
        dest = dest_of(n)
        for k, at in enumerate((low_at, high_at)):
            act(dest == me, st_do.at[n, pl.ds(k * rows, rows), :], do_all.at[pl.ds(at, rows), :],
                do_send.at[n, k], do_recv.at[chip, k], dest)

    def do_loop(lo, hi):
        def do_step(n, carry):
            @pl.when(n + WO_DEPTH - 1 < n_dest)
            def _():
                wo_copy(n + WO_DEPTH - 1).start()
            wo_copy(n).wait()

            @pl.when(n > lo)
            def _():
                do_ship(n - 1, ship_start)
            st_do[n] = lax.dot_general(dys[...], wo_buf[lax.rem(n, WO_DEPTH)], CONTRACT_LAST,
                                       preferred_element_type=F32).astype(BF16)
            return carry
        lax.fori_loop(lo, hi, do_step, 0)

    do_loop(0, DO_FIRST)
    swaps[2].wait()
    swaps[3].wait()

    def w2_copy(s):
        part = lax.rem(s, n_chunk)
        kind = s // n_chunk
        group = jnp.where(kind == 0, 0, 1 + lax.rem(kind - 1 + chip // 2, 2))
        slot = lax.rem(s, DEPTH)
        return pltpu.make_async_copy(w2_buf.at[slot], w2_all.at[group * n_chunk + part], w2_sem.at[slot])

    def w_step(s, first):
        w_start(s + DEPTH - 1)
        w_wait(s)

        @pl.when(s >= 1)
        def _():
            w2_copy(s - 1).start()

        @pl.when(s >= DEPTH)
        def _():
            w2_copy(s - DEPTH).wait()
        part = lax.rem(s, n_chunk)
        w_tile = w_buf[lax.rem(s, DEPTH)].reshape(D_CHUNK, tile_w)
        w2_buf[lax.rem(s, DEPTH)] = w_tile
        add = jnp.dot(xs[:, pl.ds(al(part * D_CHUNK, D_CHUNK), D_CHUNK)], w_tile,
                      preferred_element_type=F32)
        p_acc[...] = add if first else p_acc[...] + add

    def w_loop(lo, hi):
        def body(s, carry):
            w_step(s, False)
            return carry
        lax.fori_loop(lo, hi, body, 0)

    def kv_ship(n, act):
        dest_chip = lax.rem(n + chip, n_chip)
        dest = 2 * dest_chip + core
        lanes = pl.ds(al(dest_chip * head, head), head)
        for k, at in enumerate((low_at, high_at)):
            act(dest == me, st_kv.at[pl.ds(k * rows, rows), lanes], kv_all.at[core, pl.ds(at, rows), :],
                kv_send.at[dest_chip, k], kv_recv.at[chip, k], dest)

    def q_ship(n, act):
        t = n // 4
        dest = 4 * tile_of(t) + lax.rem(n + 2 * chip, 4)
        lanes = pl.ds(al(lax.rem(dest, 4) * wide, wide), wide)
        for k, at in enumerate((low_at, high_at)):
            act(dest == me, st_q.at[t, pl.ds(k * rows, rows), lanes], q_all.at[pl.ds(at, rows), :],
                q_send.at[n, k], q_recv.at[chip, k], dest)

    w_step(jnp.int32(0), True)
    do_ship(jnp.int32(DO_FIRST - 1), ship_start)
    w_loop(1, n_chunk)
    st_kv[...] = p_acc[...].astype(BF16)
    w_step(jnp.int32(n_chunk), True)
    each(0, n_chip, kv_ship, ship_start)
    w_loop(n_chunk + 1, 2 * n_chunk)
    st_q[0] = p_acc[...].astype(BF16)
    w_step(jnp.int32(2 * n_chunk), True)
    each(0, 4, q_ship, ship_start)
    w_loop(2 * n_chunk + 1, 3 * n_chunk)
    st_q[1] = p_acc[...].astype(BF16)
    w2_copy(jnp.int32(3 * n_chunk - 1)).start()

    def kv_arrive(src_chip, carry):
        @pl.when(src_chip != chip)
        def _():
            for k in range(2):
                rcopy(st_kv.at[pl.ds(0, rows), pl.ds(0, head)], kv_all.at[core, pl.ds(0, rows), :],
                      kv_send.at[0, k], kv_recv.at[src_chip, k], sib).wait_recv()
        return carry

    do_loop(DO_FIRST, DO_FIRST + 1)
    each(4, 8, q_ship, ship_start)
    do_ship(jnp.int32(DO_FIRST), ship_start)
    do_loop(DO_FIRST + 1, n_dest)
    for k in range(DEPTH):
        w2_copy(jnp.int32(3 * n_chunk - DEPTH + k)).wait()
    lax.fori_loop(0, n_chip, kv_arrive, 0)
    do_ship(jnp.int32(n_dest - 1), ship_start)
    each(0, n_chip, kv_ship, ship_wait)
    relay = rcopy(kv_all.at[core], kv_all.at[core], rel_send, rel_recv, sib)
    relay.start()

    def q_arrive(src_chip, carry):
        @pl.when(2 * src_chip + my_src_core != me)
        def _():
            for k in range(2):
                rcopy(st_do.at[0, pl.ds(0, rows), :], q_all.at[pl.ds(0, rows), :],
                      q_send.at[0, k], q_recv.at[src_chip, k], sib).wait_recv()
        return carry

    rcopy(kv_all.at[core], kv_all.at[1 - core], rel_send, rel_recv, sib).wait_recv()
    relay.wait_send()
    k_t[...] = kv_all[0].T
    v_t[...] = kv_all[1].T
    each(0, 8, q_ship, ship_wait)
    lax.fori_loop(0, n_chip, q_arrive, 0)

    def chunks_of(qb):
        cuts = list(range(0, qb * BQ, BK)) + [qb * BQ, (qb + 1) * BQ]
        return [slice(lo, hi) for lo, hi in zip(cuts[:-1], cuts[1:])]

    def s_at(ks):
        return slice(ks.start // BQ, ks.stop // BQ)

    def p_rows(qb, ks):
        base = BQ * (qb * (qb + 1) // 2)
        return slice(base + ks.start, base + ks.stop)

    def forward(qb):
        q_rows = slice(qb * BQ, (qb + 1) * BQ)
        q = [q_all[q_rows, h * head:(h + 1) * head] for h in range(heads)]
        chunks = chunks_of(qb)
        tops = [[] for _ in range(heads)]
        sums = [[] for _ in range(heads)]
        for ks in chunks:
            k_blk = kv_all[0, ks, :]
            for h in range(heads):
                s = lax.dot_general(k_blk, q[h], CONTRACT_LAST, preferred_element_type=F32)
                if ks.start == qb * BQ:
                    k_pos = lax.broadcasted_iota(jnp.int32, (BQ, BQ), 0)
                    q_pos = lax.broadcasted_iota(jnp.int32, (BQ, BQ), 1)
                    s = jnp.where(k_pos <= q_pos, s, -jnp.inf)
                top = jnp.max(s, axis=0, keepdims=True) * to_log2
                e = jnp.exp2(s * to_log2 - top)
                acc[s_at(ks), :, h * BQ:(h + 1) * BQ] = e.reshape(-1, BQ, BQ)
                tops[h].append(top)
                sums[h].append(jnp.sum(e, axis=0, keepdims=True))
        for h in range(heads):
            top = functools.reduce(jnp.maximum, tops[h])
            lift = [jnp.exp2(t - top) for t in tops[h]]
            inv = 1.0 / sum(a * b for a, b in zip(lift, sums[h]))
            o_t = None
            for ks, up in zip(chunks, lift):
                p = (acc[s_at(ks), :, h * BQ:(h + 1) * BQ].reshape(-1, BQ) * (up * inv)).astype(BF16)
                p_all[h, p_rows(qb, ks), :] = p
                part = jnp.dot(v_t[:, ks], p, preferred_element_type=F32)
                o_t = part if o_t is None else o_t + part
            o_all[h, :, q_rows] = o_t.astype(BF16)

    def backward(qb):
        q_rows = slice(qb * BQ, (qb + 1) * BQ)
        q = [q_all[q_rows, h * head:(h + 1) * head] for h in range(heads)]
        do = [do_all[q_rows, h * head:(h + 1) * head] for h in range(heads)]
        delta = [jnp.sum(do[h].astype(F32).T * o_all[h, :, q_rows].astype(F32), axis=0, keepdims=True)
                 for h in range(heads)]
        dq_t = [None] * heads
        for ks in chunks_of(qb):
            v_blk = kv_all[1, ks, :]
            dk = dv = None
            for h in range(heads):
                p = p_all[h, p_rows(qb, ks), :]
                dp = lax.dot_general(v_blk, do[h], CONTRACT_LAST, preferred_element_type=F32)
                ds = (p.astype(F32) * (dp - delta[h])).astype(BF16)
                part = jnp.dot(k_t[:, ks], ds, preferred_element_type=F32)
                dq_t[h] = part if dq_t[h] is None else dq_t[h] + part
                dk_h = jnp.dot(ds, q[h], preferred_element_type=F32)
                dv_h = jnp.dot(p, do[h], preferred_element_type=F32)
                dk = dk_h if dk is None else dk + dk_h
                dv = dv_h if dv is None else dv + dv_h
            dkv_acc[0, ks, :] += dk
            dkv_acc[1, ks, :] += dv
        for h in range(heads):
            dq_st[q_rows, h * head:(h + 1) * head] = (dq_t[h] * scale).T.astype(BF16)

    def block_at(step):
        side = lax.rem(lax.rem(chip, 4) // 2 + step // 4, 2)
        spot = lax.rem(step + lax.rem(chip, 2) + 2 * (chip // 4), 4)
        return jnp.where(spot < 2, 2 * spot + side, 11 - 2 * spot - side)

    def home_of(block):
        return jnp.where(block < n_chip, block, 2 * n_chip - 1 - block)

    def ahead(step, carry):
        qb = block_at(step)
        for which in range(n_block):
            @pl.when(qb == which)
            def _():
                forward(which)
        return carry

    lax.fori_loop(0, n_block, ahead, 0)

    src_slot = lax.rem(me, n_dest)

    def dq_ship(block, act):
        k = block // n_chip
        dest = 2 * home_of(block) + my_src_core
        act(dest == me, dq_st.at[pl.ds(al(block * rows, rows), rows), :],
            dq_in.at[src_slot // 4, pl.ds(al(k * rows, rows), rows), pl.ds(al(lax.rem(src_slot, 4) * wide, wide), wide)],
            dq_send.at[block], dq_recv.at[src_slot, k], dest)

    def do_done(n, carry):
        @pl.when(dest_of(n) == me)
        def _():
            do_ship(n, ship_wait)
        return carry

    lax.fori_loop(0, n_dest, do_done, 0)

    def back(step, carry):
        qb = block_at(step)
        for i in range(per):
            block = qb * per + i
            home = home_of(block)

            @pl.when(2 * home + my_src_core != me)
            def _():
                rcopy(st_do.at[0, pl.ds(0, rows), :], do_all.at[pl.ds(0, rows), :],
                      do_send.at[0, 0], do_recv.at[home, block // n_chip], sib).wait_recv()
        for which in range(n_block):
            @pl.when(qb == which)
            def _():
                backward(which)
        for i in range(per):
            dq_ship(qb * per + i, ship_start)
        return carry

    lax.fori_loop(0, n_block, back, 0)
    swap = rcopy(dkv_acc.at[1 - core], dkv_far, red_send, red_recv, sib)
    swap.start()

    def stream_copy(u):
        group = jnp.where(u < 2 * n_chunk, 1 + lax.rem(u, 2), 0)
        part = jnp.where(u < 2 * n_chunk, u // 2, u - 2 * n_chunk)
        slot = lax.rem(u, DEPTH)
        return pltpu.make_async_copy(w2_all.at[group * n_chunk + part], w2_buf.at[slot], w2_sem.at[slot])

    for u in range(DEPTH - 1):
        stream_copy(jnp.int32(u)).start()

    def do_sent(n, carry):
        @pl.when(dest_of(n) != me)
        def _():
            do_ship(n, ship_wait)
        return carry

    lax.fori_loop(0, n_dest, do_sent, 0)

    def dkv_ship(n, act):
        dest_chip = lax.rem(chip + n, n_chip)
        dest = 2 * dest_chip + core
        for k in range(2):
            block = dest_chip if k == 0 else 2 * n_chip - 1 - dest_chip
            act(dest == me, dkv_st.at[pl.ds(al(block * rows, rows), rows), :],
                dkv_in.at[pl.ds(k * rows, rows), pl.ds(al(chip * head, head), head)],
                dkv_send.at[n, k], dkv_recv.at[chip, k], dest)

    swap.wait()
    factor = jnp.where(core == 0, scale, 1.0).astype(F32)
    dkv_st[...] = ((dkv_acc[core] + dkv_far[...]) * factor).astype(BF16)
    each(0, n_block * per, dq_ship, ship_wait)
    each(0, n_chip, dkv_ship, ship_start)

    def dq_arrive(src, carry):
        @pl.when(n_dest * core + src != me)
        def _():
            for k in range(2):
                rcopy(dq_st.at[pl.ds(0, rows), :], dq_in.at[0, pl.ds(0, rows), pl.ds(0, wide)],
                      dq_send.at[0], dq_recv.at[src, k], sib).wait_recv()
        return carry

    lax.fori_loop(0, n_dest, dq_arrive, 0)

    def matmul(act, u):
        @pl.when(u + DEPTH - 1 < 3 * n_chunk)
        def _():
            stream_copy(u + DEPTH - 1).start()
        stream_copy(u).wait()
        return lax.dot_general(act, w2_buf[lax.rem(u, DEPTH)], CONTRACT_LAST, preferred_element_type=F32)

    def first_pass(part, carry):
        acc[part] = matmul(dq_in[0], 2 * part)
        acc[part] += matmul(dq_in[1], 2 * part + 1)
        return carry

    lax.fori_loop(0, n_chunk, first_pass, 0)
    each(0, n_chip, dkv_ship, ship_wait)

    def dkv_arrive(src_chip, carry):
        @pl.when(src_chip != chip)
        def _():
            for k in range(2):
                rcopy(dkv_st.at[pl.ds(0, rows), :], dkv_in.at[pl.ds(0, rows), pl.ds(0, head)],
                      dkv_send.at[0, k], dkv_recv.at[src_chip, k], sib).wait_recv()
        return carry

    lax.fori_loop(0, n_chip, dkv_arrive, 0)

    sib_low = al((1 - core) * seg, seg)
    sib_high = al(rows + core * seg, seg)

    def far_copy(part, k):
        src_at = sib_low if k == 0 else sib_high
        return rcopy(acc.at[part, pl.ds(src_at, seg), :], far.at[part, pl.ds(k * seg, seg), :],
                     far_send.at[part, k], far_recv.at[part, k], sib)

    def last_pass(part, carry):
        acc[part] += matmul(dkv_in[...], 2 * n_chunk + part)

        @pl.when(part > 0)
        def _():
            for k in range(2):
                far_copy(part - 1, k).start()
        return carry

    lax.fori_loop(0, n_chunk, last_pass, 0)
    for k in range(2):
        far_copy(n_chunk - 1, k).start()

    def finish(part, carry):
        for k in range(2):
            far_copy(part, k).wait()
        lanes = pl.ds(al(part * D_CHUNK, D_CHUNK), D_CHUNK)
        dx_ref[pl.ds(0, seg), lanes] = (acc[part, pl.ds(my_low, seg), :] + far[part, pl.ds(0, seg), :]).astype(BF16)
        dx_ref[pl.ds(seg, seg), lanes] = (acc[part, pl.ds(my_high, seg), :] + far[part, pl.ds(seg, seg), :]).astype(BF16)
        return carry

    lax.fori_loop(0, n_chunk, finish, 0)


def solution(mesh):
    n_dev = mesh.shape["cp"]
    n_chip = n_dev // 2
    row_spec = P(("dp", "cp"), None)
    any_spec = pl.BlockSpec(memory_space=pl.ANY)
    vmem_spec = pl.BlockSpec(memory_space=pltpu.VMEM)
    dma = pltpu.SemaphoreType.DMA

    def device_fn(x_in, d_y, w_q, w_k, w_v, w_o):
        rows, d_model = x_in.shape
        q_heads, head = w_q.shape[1], w_q.shape[2]
        kv_heads = w_k.shape[1]
        seq = rows * n_dev
        scale = head ** -0.5
        wide = q_heads // n_dev * head
        tile_w = kv_heads * head
        n_chunk = d_model // D_CHUNK
        wo_flat = w_o.reshape(q_heads * head, d_model)
        params = functools.partial(pltpu.CompilerParams, vmem_limit_bytes=VMEM_LIMIT)
        tri = (seq // BQ) * (seq // BQ + 1) // 2 * BQ
        return pl.pallas_call(
            functools.partial(fused_kernel, n_dev, scale),
            out_shape=(jax.ShapeDtypeStruct((rows, d_model), BF16),
                       jax.ShapeDtypeStruct((3 * n_chunk, D_CHUNK, tile_w), BF16)),
            in_specs=[vmem_spec, vmem_spec, any_spec, any_spec, any_spec, any_spec],
            out_specs=(vmem_spec, any_spec),
            scratch_shapes=[
                pltpu.VMEM((2 * rows, d_model), BF16),
                pltpu.VMEM((2 * rows, d_model), BF16),
                pltpu.VMEM((WO_DEPTH, wide, d_model), BF16),
                pltpu.VMEM((DEPTH, D_CHUNK, kv_heads, head), BF16),
                pltpu.VMEM((DEPTH, D_CHUNK, tile_w), BF16),
                pltpu.VMEM((2 * rows, tile_w), F32),
                pltpu.VMEM((n_chip, 2 * rows, wide), BF16),
                pltpu.VMEM((2 * rows, tile_w), BF16),
                pltpu.VMEM((2, 2 * rows, tile_w), BF16),
                pltpu.VMEM((seq, wide), BF16),
                pltpu.VMEM((seq, wide), BF16),
                pltpu.VMEM((2, seq, head), BF16),
                pltpu.VMEM((head, seq), BF16),
                pltpu.VMEM((head, seq), BF16),
                pltpu.VMEM((wide // head, tri, BQ), BF16),
                pltpu.VMEM((wide // head, head, seq), BF16),
                pltpu.VMEM((seq, wide), BF16),
                pltpu.VMEM((2, seq, head), F32),
                pltpu.VMEM((2, 2 * rows, tile_w), BF16),
                pltpu.VMEM((2 * rows, tile_w), BF16),
                pltpu.VMEM((seq, head), F32),
                pltpu.VMEM((seq, head), BF16),
                pltpu.VMEM((n_chunk, 2 * rows, D_CHUNK), F32),
                pltpu.VMEM((n_chunk, rows, D_CHUNK), F32),
                dma((WO_DEPTH,)), dma((DEPTH,)), dma((DEPTH,)), dma((2, 2)), dma((2, 2)),
                dma((n_chip, 2)), dma((n_chip, 2)), dma((n_chip, 2)), dma((n_chip, 2)),
                dma((n_chip, 2)), dma((n_chip, 2)), dma, dma,
                dma((seq // rows,)), dma((n_chip, 2)), dma((n_chip, 2)), dma((n_chip, 2)),
                dma((n_chunk, 2)), dma((n_chunk, 2)), dma, dma,
            ],
            compiler_params=params(collective_id=0, has_side_effects=True),
            name="fused",
        )(x_in, d_y, w_q, w_k, w_v, wo_flat)[0]

    return jax.shard_map(device_fn, mesh=mesh, in_specs=(row_spec, row_spec, P(), P(), P(), P()),
                         out_specs=row_spec, check_vma=False)
```

time: 140 us -> 132 us (0.943)
  Pallas kernels: 137 us -> 129 us
    pallas_call x2 -> x1, Pallas kernels: 137 us -> 129 us  [device_fn(): pl.pallas_call(functools.partial(fused_kernel, n_dev, scale), out_shape=(...]
where the time goes in v3:
time: 132 us
  Pallas kernels  129 us (98%)
  local copies, waits for them, and re-layouts  2.46 us (2%)
    pallas_call x1, Pallas kernels, device_fn(): pl.pallas_call(functools.partial(fused_kernel, n_dev, scale), out_shape=(...  129 us

profile of v3, /device:TPU:21, one launch (start us, length us, event | category | flops | bytes accessed | tf_op | source)
XLA Modules:
  0.0 131.7 jit_solution(6795836432275309061)
XLA Ops:
  0.0 129.2 %fused.1 = (bf16[128,5120]{1,0:T(8,128)(2,1)}, bf16[30,512,1024]{2,1,0:T(8,128)(2,1)}) custom-call(bf16[128,5120]{1,0:T(8,128)(2,1)} %x_ref.1, bf16[128,5120]{1,0:T(8,128)(2,1)} %dy_ref.1, bf16[5120,32,128]{2,1,0:T(8,128)(2,1)} %wq.1, bf16[5120,8,128]{2,1,0:T(8,128)(2,1)} %wk.1, bf16[5120,8,128]{2,1,0:T(8,128)(2,1)} %wv.1, bf16[4096,5120]{1,0:T(8,128)(2,1)} %bitcast.1), custom_call_target="tpu_custom_call" | custom-call | tf_op jit(solution)/shard_map/fused/pallas_call | solution.py:526
  129.2 2.5 %copy.8 = bf16[128,5120]{1,0:T(8,128)(2,1)} copy(bf16[128,5120]{1,0:T(8,128)(2,1)} %get-tuple-element.6) | data formatting | bytes 2621440

commit v4 on v3

--- a/solution.py
+++ b/solution.py
@@ -12,6 +12,7 @@
 F32 = jnp.float32
 CONTRACT_LAST = (((1,), (1,)), ((), ()))
 DEPTH = 4
+W2_DEPTH = 6
 WO_DEPTH = 2
 D_CHUNK = 512
 BQ = 256
@@ -73,7 +74,7 @@
 def fused_kernel(n_dev, scale, x_ref, dy_ref, wq, wk, wv, wo, dx_ref, w2_all,
                  xs, dys, wo_buf, w_buf, w2_buf, p_acc, st_do, st_kv, st_q,
                  q_all, do_all, kv_all, k_t, v_t, p_all, o_all, dq_st, dkv_acc,
-                 dq_in, dkv_in, dkv_far, dkv_st, acc, far,
+                 dq_in, dkv_in, dkv_far, dkv_st, grads_t, acc, far,
                  wo_sem, w_sem, w2_sem, x_send, x_recv, do_send, do_recv,
                  kv_send, kv_recv, q_send, q_recv, rel_send, rel_recv,
                  dq_send, dq_recv, dkv_send, dkv_recv, far_send, far_recv, red_send, red_recv):
@@ -96,7 +97,9 @@
     to_log2 = scale * 1.4426950408889634
 
     def dest_of(n):
-        return n_dest * core + lax.rem(2 * n_chip + 2 * chip - 2 * (n // 2) + lax.rem(n, 2), n_dest)
+        spot, step = lax.rem(chip, 4), n // 2
+        flip = 2 * lax.rem(spot // 2 + step // 2, 2) + lax.rem(spot + step, 2)
+        return n_dest * core + 2 * flip + lax.rem(n, 2)
 
     def wo_copy(n):
         return pltpu.make_async_copy(
@@ -165,22 +168,23 @@
             act(dest == me, st_do.at[n, pl.ds(k * rows, rows), :], do_all.at[pl.ds(at, rows), :],
                 do_send.at[n, k], do_recv.at[chip, k], dest)
 
-    def do_loop(lo, hi):
+    def do_loop(lo, hi, send):
         def do_step(n, carry):
             @pl.when(n + WO_DEPTH - 1 < n_dest)
             def _():
                 wo_copy(n + WO_DEPTH - 1).start()
             wo_copy(n).wait()
 
-            @pl.when(n > lo)
-            def _():
-                do_ship(n - 1, ship_start)
+            if send:
+                @pl.when(n > lo)
+                def _():
+                    do_ship(n - 1, ship_start)
             st_do[n] = lax.dot_general(dys[...], wo_buf[lax.rem(n, WO_DEPTH)], CONTRACT_LAST,
                                        preferred_element_type=F32).astype(BF16)
             return carry
         lax.fori_loop(lo, hi, do_step, 0)
 
-    do_loop(0, DO_FIRST)
+    do_loop(0, DO_FIRST, True)
     swaps[2].wait()
     swaps[3].wait()
 
@@ -188,7 +192,7 @@
         part = lax.rem(s, n_chunk)
         kind = s // n_chunk
         group = jnp.where(kind == 0, 0, 1 + lax.rem(kind - 1 + chip // 2, 2))
-        slot = lax.rem(s, DEPTH)
+        slot = lax.rem(s, W2_DEPTH)
         return pltpu.make_async_copy(w2_buf.at[slot], w2_all.at[group * n_chunk + part], w2_sem.at[slot])
 
     def w_step(s, first):
@@ -199,12 +203,12 @@
         def _():
             w2_copy(s - 1).start()
 
-        @pl.when(s >= DEPTH)
-        def _():
-            w2_copy(s - DEPTH).wait()
+        @pl.when(s >= W2_DEPTH)
+        def _():
+            w2_copy(s - W2_DEPTH).wait()
         part = lax.rem(s, n_chunk)
         w_tile = w_buf[lax.rem(s, DEPTH)].reshape(D_CHUNK, tile_w)
-        w2_buf[lax.rem(s, DEPTH)] = w_tile
+        w2_buf[lax.rem(s, W2_DEPTH)] = w_tile
         add = jnp.dot(xs[:, pl.ds(al(part * D_CHUNK, D_CHUNK), D_CHUNK)], w_tile,
                       preferred_element_type=F32)
         p_acc[...] = add if first else p_acc[...] + add
@@ -253,32 +257,21 @@
                       kv_send.at[0, k], kv_recv.at[src_chip, k], sib).wait_recv()
         return carry
 
-    do_loop(DO_FIRST, DO_FIRST + 1)
+    do_loop(DO_FIRST, DO_FIRST + 1, False)
     each(4, 8, q_ship, ship_start)
-    do_ship(jnp.int32(DO_FIRST), ship_start)
-    do_loop(DO_FIRST + 1, n_dest)
-    for k in range(DEPTH):
-        w2_copy(jnp.int32(3 * n_chunk - DEPTH + k)).wait()
+    do_loop(DO_FIRST + 1, n_dest, False)
+    for k in range(W2_DEPTH):
+        w2_copy(jnp.int32(3 * n_chunk - W2_DEPTH + k)).wait()
     lax.fori_loop(0, n_chip, kv_arrive, 0)
-    do_ship(jnp.int32(n_dest - 1), ship_start)
     each(0, n_chip, kv_ship, ship_wait)
     relay = rcopy(kv_all.at[core], kv_all.at[core], rel_send, rel_recv, sib)
     relay.start()
-
-    def q_arrive(src_chip, carry):
-        @pl.when(2 * src_chip + my_src_core != me)
-        def _():
-            for k in range(2):
-                rcopy(st_do.at[0, pl.ds(0, rows), :], q_all.at[pl.ds(0, rows), :],
-                      q_send.at[0, k], q_recv.at[src_chip, k], sib).wait_recv()
-        return carry
-
     rcopy(kv_all.at[core], kv_all.at[1 - core], rel_send, rel_recv, sib).wait_recv()
     relay.wait_send()
     k_t[...] = kv_all[0].T
     v_t[...] = kv_all[1].T
-    each(0, 8, q_ship, ship_wait)
-    lax.fori_loop(0, n_chip, q_arrive, 0)
+    each(0, 4, q_ship, ship_wait)
+    each(DO_FIRST, 4, do_ship, ship_start)
 
     def chunks_of(qb):
         cuts = list(range(0, qb * BQ, BK)) + [qb * BQ, (qb + 1) * BQ]
@@ -307,7 +300,7 @@
                     s = jnp.where(k_pos <= q_pos, s, -jnp.inf)
                 top = jnp.max(s, axis=0, keepdims=True) * to_log2
                 e = jnp.exp2(s * to_log2 - top)
-                acc[s_at(ks), :, h * BQ:(h + 1) * BQ] = e.reshape(-1, BQ, BQ)
+                acc[s_at(ks), h * BQ:(h + 1) * BQ, :] = e.reshape(-1, BQ, BQ)
                 tops[h].append(top)
                 sums[h].append(jnp.sum(e, axis=0, keepdims=True))
         for h in range(heads):
@@ -316,7 +309,7 @@
             inv = 1.0 / sum(a * b for a, b in zip(lift, sums[h]))
             o_t = None
             for ks, up in zip(chunks, lift):
-                p = (acc[s_at(ks), :, h * BQ:(h + 1) * BQ].reshape(-1, BQ) * (up * inv)).astype(BF16)
+                p = (acc[s_at(ks), h * BQ:(h + 1) * BQ, :].reshape(-1, BQ) * (up * inv)).astype(BF16)
                 p_all[h, p_rows(qb, ks), :] = p
                 part = jnp.dot(v_t[:, ks], p, preferred_element_type=F32)
                 o_t = part if o_t is None else o_t + part
@@ -357,6 +350,19 @@
 
     def ahead(step, carry):
         qb = block_at(step)
+
+        @pl.when(step == n_block // 2)
+        def _():
+            each(4, 8, q_ship, ship_wait)
+            each(4, n_dest, do_ship, ship_start)
+        for i in range(per):
+            block = qb * per + i
+            home = home_of(block)
+
+            @pl.when(2 * home + my_src_core != me)
+            def _():
+                rcopy(st_do.at[0, pl.ds(0, rows), :], q_all.at[pl.ds(0, rows), :],
+                      q_send.at[0, 0], q_recv.at[home, block // n_chip], sib).wait_recv()
         for which in range(n_block):
             @pl.when(qb == which)
             def _():
@@ -407,10 +413,10 @@
     def stream_copy(u):
         group = jnp.where(u < 2 * n_chunk, 1 + lax.rem(u, 2), 0)
         part = jnp.where(u < 2 * n_chunk, u // 2, u - 2 * n_chunk)
-        slot = lax.rem(u, DEPTH)
+        slot = lax.rem(u, W2_DEPTH)
         return pltpu.make_async_copy(w2_all.at[group * n_chunk + part], w2_buf.at[slot], w2_sem.at[slot])
 
-    for u in range(DEPTH - 1):
+    for u in range(W2_DEPTH - 1):
         stream_copy(jnp.int32(u)).start()
 
     def do_sent(n, carry):
@@ -433,8 +439,8 @@
     swap.wait()
     factor = jnp.where(core == 0, scale, 1.0).astype(F32)
     dkv_st[...] = ((dkv_acc[core] + dkv_far[...]) * factor).astype(BF16)
+    each(0, n_chip, dkv_ship, ship_start)
     each(0, n_block * per, dq_ship, ship_wait)
-    each(0, n_chip, dkv_ship, ship_start)
 
     def dq_arrive(src, carry):
         @pl.when(n_dest * core + src != me)
@@ -446,16 +452,22 @@
 
     lax.fori_loop(0, n_dest, dq_arrive, 0)
 
-    def matmul(act, u):
-        @pl.when(u + DEPTH - 1 < 3 * n_chunk)
-        def _():
-            stream_copy(u + DEPTH - 1).start()
+    def by_token(x):
+        return jnp.concatenate([x[:seg], x[3 * seg:], x[seg:3 * seg]], axis=0).T
+
+    def matmul(group, u):
+        @pl.when(u + W2_DEPTH - 1 < 3 * n_chunk)
+        def _():
+            stream_copy(u + W2_DEPTH - 1).start()
         stream_copy(u).wait()
-        return lax.dot_general(act, w2_buf[lax.rem(u, DEPTH)], CONTRACT_LAST, preferred_element_type=F32)
+        return jnp.dot(w2_buf[lax.rem(u, W2_DEPTH)], grads_t[group], preferred_element_type=F32)
+
+    grads_t[0] = by_token(dq_in[0])
+    grads_t[1] = by_token(dq_in[1])
 
     def first_pass(part, carry):
-        acc[part] = matmul(dq_in[0], 2 * part)
-        acc[part] += matmul(dq_in[1], 2 * part + 1)
+        acc[part] = matmul(0, 2 * part)
+        acc[part] += matmul(1, 2 * part + 1)
         return carry
 
     lax.fori_loop(0, n_chunk, first_pass, 0)
@@ -471,33 +483,27 @@
 
     lax.fori_loop(0, n_chip, dkv_arrive, 0)
 
-    sib_low = al((1 - core) * seg, seg)
-    sib_high = al(rows + core * seg, seg)
-
-    def far_copy(part, k):
-        src_at = sib_low if k == 0 else sib_high
-        return rcopy(acc.at[part, pl.ds(src_at, seg), :], far.at[part, pl.ds(k * seg, seg), :],
-                     far_send.at[part, k], far_recv.at[part, k], sib)
+    grads_t[2] = by_token(dkv_in[...])
+    my_lanes = pl.ds(al(core * rows, rows), rows)
+    sib_lanes = pl.ds(al((1 - core) * rows, rows), rows)
+
+    def far_copy(part):
+        return rcopy(acc.at[part, :, sib_lanes], far.at[part], far_send.at[part], far_recv.at[part], sib)
 
     def last_pass(part, carry):
-        acc[part] += matmul(dkv_in[...], 2 * n_chunk + part)
+        acc[part] += matmul(2, 2 * n_chunk + part)
 
         @pl.when(part > 0)
         def _():
-            for k in range(2):
-                far_copy(part - 1, k).start()
+            far_copy(part - 1).start()
         return carry
 
     lax.fori_loop(0, n_chunk, last_pass, 0)
-    for k in range(2):
-        far_copy(n_chunk - 1, k).start()
+    far_copy(n_chunk - 1).start()
 
     def finish(part, carry):
-        for k in range(2):
-            far_copy(part, k).wait()
-        lanes = pl.ds(al(part * D_CHUNK, D_CHUNK), D_CHUNK)
-        dx_ref[pl.ds(0, seg), lanes] = (acc[part, pl.ds(my_low, seg), :] + far[part, pl.ds(0, seg), :]).astype(BF16)
-        dx_ref[pl.ds(seg, seg), lanes] = (acc[part, pl.ds(my_high, seg), :] + far[part, pl.ds(seg, seg), :]).astype(BF16)
+        far_copy(part).wait()
+        dx_ref[:, pl.ds(al(part * D_CHUNK, D_CHUNK), D_CHUNK)] = (acc[part, :, my_lanes] + far[part]).astype(BF16).T
         return carry
 
     lax.fori_loop(0, n_chunk, finish, 0)
@@ -534,7 +540,7 @@
                 pltpu.VMEM((2 * rows, d_model), BF16),
                 pltpu.VMEM((WO_DEPTH, wide, d_model), BF16),
                 pltpu.VMEM((DEPTH, D_CHUNK, kv_heads, head), BF16),
-                pltpu.VMEM((DEPTH, D_CHUNK, tile_w), BF16),
+                pltpu.VMEM((W2_DEPTH, D_CHUNK, tile_w), BF16),
                 pltpu.VMEM((2 * rows, tile_w), F32),
                 pltpu.VMEM((n_chip, 2 * rows, wide), BF16),
                 pltpu.VMEM((2 * rows, tile_w), BF16),
@@ -552,13 +558,14 @@
                 pltpu.VMEM((2 * rows, tile_w), BF16),
                 pltpu.VMEM((seq, head), F32),
                 pltpu.VMEM((seq, head), BF16),
-                pltpu.VMEM((n_chunk, 2 * rows, D_CHUNK), F32),
-                pltpu.VMEM((n_chunk, rows, D_CHUNK), F32),
-                dma((WO_DEPTH,)), dma((DEPTH,)), dma((DEPTH,)), dma((2, 2)), dma((2, 2)),
+                pltpu.VMEM((3, tile_w, 2 * rows), BF16),
+                pltpu.VMEM((n_chunk, D_CHUNK, 2 * rows), F32),
+                pltpu.VMEM((n_chunk, D_CHUNK, rows), F32),
+                dma((WO_DEPTH,)), dma((DEPTH,)), dma((W2_DEPTH,)), dma((2, 2)), dma((2, 2)),
                 dma((n_chip, 2)), dma((n_chip, 2)), dma((n_chip, 2)), dma((n_chip, 2)),
                 dma((n_chip, 2)), dma((n_chip, 2)), dma, dma,
                 dma((seq // rows,)), dma((n_chip, 2)), dma((n_chip, 2)), dma((n_chip, 2)),
-                dma((n_chunk, 2)), dma((n_chunk, 2)), dma, dma,
+                dma((n_chunk,)), dma((n_chunk,)), dma, dma,
             ],
             compiler_params=params(collective_id=0, has_side_effects=True),
             name="fused",

time: 132 us -> 136 us (1.030)
  Pallas kernels: 129 us -> 133 us
    pallas_call x1, Pallas kernels: 129 us -> 133 us  [device_fn(): pl.pallas_call(functools.partial(fused_kernel, n_dev, scale), out_shape=(...]
where the time goes in v4:
time: 136 us
  Pallas kernels  133 us (98%)
  local copies, waits for them, and re-layouts  2.46 us (2%)
    pallas_call x1, Pallas kernels, device_fn(): pl.pallas_call(functools.partial(fused_kernel, n_dev, scale), out_shape=(...  133 us

profile of v4, /device:TPU:21, one launch (start us, length us, event | category | flops | bytes accessed | tf_op | source)
XLA Modules:
  0.0 135.5 jit_solution(11153353309048193897)
XLA Ops:
  0.0 133.1 %fused.1 = (bf16[128,5120]{1,0:T(8,128)(2,1)}, bf16[30,512,1024]{2,1,0:T(8,128)(2,1)}) custom-call(bf16[128,5120]{1,0:T(8,128)(2,1)} %x_ref.1, bf16[128,5120]{1,0:T(8,128)(2,1)} %dy_ref.1, bf16[5120,32,128]{2,1,0:T(8,128)(2,1)} %wq.1, bf16[5120,8,128]{2,1,0:T(8,128)(2,1)} %wk.1, bf16[5120,8,128]{2,1,0:T(8,128)(2,1)} %wv.1, bf16[4096,5120]{1,0:T(8,128)(2,1)} %bitcast.1), custom_call_target="tpu_custom_call" | custom-call | tf_op jit(solution)/shard_map/fused/pallas_call | solution.py:532
  133.1 2.5 %copy.8 = bf16[128,5120]{1,0:T(8,128)(2,1)} copy(bf16[128,5120]{1,0:T(8,128)(2,1)} %get-tuple-element.6) | data formatting | bytes 2621440

commit v5 on v4

--- a/solution.py
+++ b/solution.py
@@ -12,7 +12,7 @@
 F32 = jnp.float32
 CONTRACT_LAST = (((1,), (1,)), ((), ()))
 DEPTH = 4
-W2_DEPTH = 6
+W2_DEPTH = 8
 WO_DEPTH = 2
 D_CHUNK = 512
 BQ = 256
@@ -410,13 +410,18 @@
     swap = rcopy(dkv_acc.at[1 - core], dkv_far, red_send, red_recv, sib)
     swap.start()
 
+    early = lax.rem(chip, 4) // 2
+    n_pair = n_chunk // 2
+    n_slot = W2_DEPTH // 2
+
     def stream_copy(u):
-        group = jnp.where(u < 2 * n_chunk, 1 + lax.rem(u, 2), 0)
-        part = jnp.where(u < 2 * n_chunk, u // 2, u - 2 * n_chunk)
-        slot = lax.rem(u, W2_DEPTH)
-        return pltpu.make_async_copy(w2_all.at[group * n_chunk + part], w2_buf.at[slot], w2_sem.at[slot])
-
-    for u in range(W2_DEPTH - 1):
+        turn = u // n_pair
+        group = jnp.where(turn == 0, 1 + early, jnp.where(turn == 1, 2 - early, 0))
+        part = group * n_chunk + 2 * lax.rem(u, n_pair)
+        slot = lax.rem(u, n_slot)
+        return pltpu.make_async_copy(w2_all.at[pl.ds(part, 2)], w2_buf.at[pl.ds(2 * slot, 2)], w2_sem.at[slot])
+
+    for u in range(n_slot - 1):
         stream_copy(jnp.int32(u)).start()
 
     def do_sent(n, carry):
@@ -440,37 +445,57 @@
     factor = jnp.where(core == 0, scale, 1.0).astype(F32)
     dkv_st[...] = ((dkv_acc[core] + dkv_far[...]) * factor).astype(BF16)
     each(0, n_chip, dkv_ship, ship_start)
-    each(0, n_block * per, dq_ship, ship_wait)
-
-    def dq_arrive(src, carry):
+
+    def dq_arrive(n, carry):
+        src = lax.rem(4 * early + n, n_dest)
+
         @pl.when(n_dest * core + src != me)
         def _():
             for k in range(2):
                 rcopy(dq_st.at[pl.ds(0, rows), :], dq_in.at[0, pl.ds(0, rows), pl.ds(0, wide)],
                       dq_send.at[0], dq_recv.at[src, k], sib).wait_recv()
-        return carry
-
-    lax.fori_loop(0, n_dest, dq_arrive, 0)
+
+        @pl.when(n_dest * core + src == me)
+        def _():
+            for k in range(2):
+                dq_ship(jnp.where(k == 0, chip, 2 * n_chip - 1 - chip), ship_wait)
+        return carry
 
     def by_token(x):
         return jnp.concatenate([x[:seg], x[3 * seg:], x[seg:3 * seg]], axis=0).T
 
     def matmul(group, u):
-        @pl.when(u + W2_DEPTH - 1 < 3 * n_chunk)
-        def _():
-            stream_copy(u + W2_DEPTH - 1).start()
+        @pl.when(u + n_slot - 1 < 3 * n_pair)
+        def _():
+            stream_copy(u + n_slot - 1).start()
         stream_copy(u).wait()
-        return jnp.dot(w2_buf[lax.rem(u, W2_DEPTH)], grads_t[group], preferred_element_type=F32)
-
-    grads_t[0] = by_token(dq_in[0])
-    grads_t[1] = by_token(dq_in[1])
-
-    def first_pass(part, carry):
-        acc[part] = matmul(0, 2 * part)
-        acc[part] += matmul(1, 2 * part + 1)
-        return carry
-
-    lax.fori_loop(0, n_chunk, first_pass, 0)
+        pair = w2_buf[pl.ds(2 * lax.rem(u, n_slot), 2)].reshape(2 * D_CHUNK, tile_w)
+        return jnp.dot(pair, grads_t[group], preferred_element_type=F32).reshape(2, D_CHUNK, 2 * rows)
+
+    lax.fori_loop(0, n_dest // 2, dq_arrive, 0)
+    grads_t[0] = by_token(dq_in[early])
+
+    def early_pass(part, carry):
+        acc[pl.ds(2 * part, 2)] = matmul(0, part)
+        return carry
+
+    lax.fori_loop(0, n_pair, early_pass, 0)
+    lax.fori_loop(n_dest // 2, n_dest, dq_arrive, 0)
+    grads_t[1] = by_token(dq_in[1 - early])
+
+    def late_pass(part, carry):
+        acc[pl.ds(2 * part, 2)] += matmul(1, n_pair + part)
+        return carry
+
+    lax.fori_loop(0, n_pair, late_pass, 0)
+
+    def dq_sent(block, carry):
+        @pl.when(2 * home_of(block) + my_src_core != me)
+        def _():
+            dq_ship(block, ship_wait)
+        return carry
+
+    lax.fori_loop(0, n_block * per, dq_sent, 0)
     each(0, n_chip, dkv_ship, ship_wait)
 
     def dkv_arrive(src_chip, carry):
@@ -488,25 +513,29 @@
     sib_lanes = pl.ds(al((1 - core) * rows, rows), rows)
 
     def far_copy(part):
-        return rcopy(acc.at[part, :, sib_lanes], far.at[part], far_send.at[part], far_recv.at[part], sib)
+        two = pl.ds(2 * part, 2)
+        return rcopy(acc.at[two, :, sib_lanes], far.at[two], far_send.at[part], far_recv.at[part], sib)
 
     def last_pass(part, carry):
-        acc[part] += matmul(2, 2 * n_chunk + part)
+        acc[pl.ds(2 * part, 2)] += matmul(2, 2 * n_pair + part)
 
         @pl.when(part > 0)
         def _():
             far_copy(part - 1).start()
         return carry
 
-    lax.fori_loop(0, n_chunk, last_pass, 0)
-    far_copy(n_chunk - 1).start()
+    lax.fori_loop(0, n_pair, last_pass, 0)
+    far_copy(n_pair - 1).start()
 
     def finish(part, carry):
         far_copy(part).wait()
-        dx_ref[:, pl.ds(al(part * D_CHUNK, D_CHUNK), D_CHUNK)] = (acc[part, :, my_lanes] + far[part]).astype(BF16).T
-        return carry
-
-    lax.fori_loop(0, n_chunk, finish, 0)
+        for k in range(2):
+            piece = 2 * part + k
+            dx_ref[:, pl.ds(al(piece * D_CHUNK, D_CHUNK), D_CHUNK)] = (
+                acc[piece, :, my_lanes] + far[piece]).astype(BF16).T
+        return carry
+
+    lax.fori_loop(0, n_pair, finish, 0)
 
 
 def solution(mesh):

time: 136 us -> 126 us (0.926)
  Pallas kernels: 133 us -> 123 us
    pallas_call x1, Pallas kernels: 133 us -> 123 us  [device_fn(): pl.pallas_call(functools.partial(fused_kernel, n_dev, scale), out_shape=(...]
where the time goes in v5:
time: 126 us; the launch traced here: 125 us
  Pallas kernels  123 us (98%)
  local copies, waits for them, and re-layouts  2.46 us (2%)
    pallas_call x1, Pallas kernels, device_fn(): pl.pallas_call(functools.partial(fused_kernel, n_dev, scale), out_shape=(...  123 us

profile of v5, /device:TPU:21, one launch (start us, length us, event | category | flops | bytes accessed | tf_op | source)
XLA Modules:
  0.0 125.2 jit_solution(16868047099164393879)
XLA Ops:
  0.0 122.7 %fused.1 = (bf16[128,5120]{1,0:T(8,128)(2,1)}, bf16[30,512,1024]{2,1,0:T(8,128)(2,1)}) custom-call(bf16[128,5120]{1,0:T(8,128)(2,1)} %x_ref.1, bf16[128,5120]{1,0:T(8,128)(2,1)} %dy_ref.1, bf16[5120,32,128]{2,1,0:T(8,128)(2,1)} %wq.1, bf16[5120,8,128]{2,1,0:T(8,128)(2,1)} %wk.1, bf16[5120,8,128]{2,1,0:T(8,128)(2,1)} %wv.1, bf16[4096,5120]{1,0:T(8,128)(2,1)} %bitcast.1), custom_call_target="tpu_custom_call" | custom-call | tf_op jit(solution)/shard_map/fused/pallas_call | solution.py:561
  122.7 2.5 %copy.8 = bf16[128,5120]{1,0:T(8,128)(2,1)} copy(bf16[128,5120]{1,0:T(8,128)(2,1)} %get-tuple-element.6) | data formatting | bytes 2621440

commit v6 on v5

--- a/solution.py
+++ b/solution.py
@@ -17,7 +17,7 @@
 D_CHUNK = 512
 BQ = 256
 BK = 512
-DO_FIRST = 2
+DO_FIRST = 4
 VMEM_LIMIT = 62 * 2 ** 20
 
 
@@ -151,10 +151,12 @@
                            x_send.at[k, 0], x_recv.at[k, 0], sib))
         swaps.append(rcopy(ref.at[pl.ds(seg, seg)], stack.at[pl.ds(my_high, seg)],
                            x_send.at[k, 1], x_recv.at[k, 1], sib))
-    for swap in swaps:
-        swap.start()
+    swaps[0].start()
+    swaps[1].start()
     swaps[0].wait()
     swaps[1].wait()
+    swaps[2].start()
+    swaps[3].start()
 
     def each(lo, hi, ship, act):
         def step(n, carry):
@@ -271,7 +273,6 @@
     k_t[...] = kv_all[0].T
     v_t[...] = kv_all[1].T
     each(0, 4, q_ship, ship_wait)
-    each(DO_FIRST, 4, do_ship, ship_start)
 
     def chunks_of(qb):
         cuts = list(range(0, qb * BQ, BK)) + [qb * BQ, (qb + 1) * BQ]
@@ -353,8 +354,13 @@
 
         @pl.when(step == n_block // 2)
         def _():
-            each(4, 8, q_ship, ship_wait)
-            each(4, n_dest, do_ship, ship_start)
+            each(4, 6, q_ship, ship_wait)
+            each(DO_FIRST, 6, do_ship, ship_start)
+
+        @pl.when(step == n_block // 2 + 1)
+        def _():
+            each(6, 8, q_ship, ship_wait)
+            each(6, n_dest, do_ship, ship_start)
         for i in range(per):
             block = qb * per + i
             home = home_of(block)

time: 126 us -> 124 us (0.984)
  Pallas kernels: 123 us -> 121 us
    pallas_call x1, Pallas kernels: 123 us -> 121 us  [device_fn(): pl.pallas_call(functools.partial(fused_kernel, n_dev, scale), out_shape=(...]
where the time goes in v6:
time: 124 us; the launch traced here: 123 us
  Pallas kernels  121 us (98%)
  local copies, waits for them, and re-layouts  2.46 us (2%)
    pallas_call x1, Pallas kernels, device_fn(): pl.pallas_call(functools.partial(fused_kernel, n_dev, scale), out_shape=(...  121 us

profile of v6, /device:TPU:21, one launch (start us, length us, event | category | flops | bytes accessed | tf_op | source)
XLA Modules:
  0.0 123.3 jit_solution(13372512913516425754)
XLA Ops:
  0.0 120.8 %fused.1 = (bf16[128,5120]{1,0:T(8,128)(2,1)}, bf16[30,512,1024]{2,1,0:T(8,128)(2,1)}) custom-call(bf16[128,5120]{1,0:T(8,128)(2,1)} %x_ref.1, bf16[128,5120]{1,0:T(8,128)(2,1)} %dy_ref.1, bf16[5120,32,128]{2,1,0:T(8,128)(2,1)} %wq.1, bf16[5120,8,128]{2,1,0:T(8,128)(2,1)} %wk.1, bf16[5120,8,128]{2,1,0:T(8,128)(2,1)} %wv.1, bf16[4096,5120]{1,0:T(8,128)(2,1)} %bitcast.1), custom_call_target="tpu_custom_call" | custom-call | tf_op jit(solution)/shard_map/fused/pallas_call | solution.py:567
  120.8 2.5 %copy.8 = bf16[128,5120]{1,0:T(8,128)(2,1)} copy(bf16[128,5120]{1,0:T(8,128)(2,1)} %get-tuple-element.6) | data formatting | bytes 2621440

commit v7 on v6

--- a/solution.py
+++ b/solution.py
@@ -97,7 +97,7 @@
     to_log2 = scale * 1.4426950408889634
 
     def dest_of(n):
-        spot, step = lax.rem(chip, 4), n // 2
+        spot, step = lax.rem(chip, 4), jnp.where(n < 4, 1 - n // 2, n // 2)
         flip = 2 * lax.rem(spot // 2 + step // 2, 2) + lax.rem(spot + step, 2)
         return n_dest * core + 2 * flip + lax.rem(n, 2)
 
@@ -222,7 +222,7 @@
         lax.fori_loop(lo, hi, body, 0)
 
     def kv_ship(n, act):
-        dest_chip = lax.rem(n + chip, n_chip)
+        dest_chip = lax.rem(n + 1 + chip, n_chip)
         dest = 2 * dest_chip + core
         lanes = pl.ds(al(dest_chip * head, head), head)
         for k, at in enumerate((low_at, high_at)):
@@ -231,7 +231,7 @@
 
     def q_ship(n, act):
         t = n // 4
-        dest = 4 * tile_of(t) + lax.rem(n + 2 * chip, 4)
+        dest = 4 * tile_of(t) + lax.rem(n + 2 + 2 * chip, 4)
         lanes = pl.ds(al(lax.rem(dest, 4) * wide, wide), wide)
         for k, at in enumerate((low_at, high_at)):
             act(dest == me, st_q.at[t, pl.ds(k * rows, rows), lanes], q_all.at[pl.ds(at, rows), :],
@@ -522,26 +522,25 @@
         two = pl.ds(2 * part, 2)
         return rcopy(acc.at[two, :, sib_lanes], far.at[two], far_send.at[part], far_recv.at[part], sib)
 
-    def last_pass(part, carry):
-        acc[pl.ds(2 * part, 2)] += matmul(2, 2 * n_pair + part)
-
-        @pl.when(part > 0)
-        def _():
-            far_copy(part - 1).start()
-        return carry
-
-    lax.fori_loop(0, n_pair, last_pass, 0)
-    far_copy(n_pair - 1).start()
-
-    def finish(part, carry):
+    def finish(part):
         far_copy(part).wait()
         for k in range(2):
             piece = 2 * part + k
             dx_ref[:, pl.ds(al(piece * D_CHUNK, D_CHUNK), D_CHUNK)] = (
                 acc[piece, :, my_lanes] + far[piece]).astype(BF16).T
-        return carry
-
-    lax.fori_loop(0, n_pair, finish, 0)
+
+    def last_pass(part, carry):
+        acc[pl.ds(2 * part, 2)] += matmul(2, 2 * n_pair + part)
+
+        @pl.when(part > 1)
+        def _():
+            finish(part - 2)
+        far_copy(part).start()
+        return carry
+
+    lax.fori_loop(0, n_pair, last_pass, 0)
+    finish(n_pair - 2)
+    finish(n_pair - 1)
 
 
 def solution(mesh):

time: 124 us -> 122 us (0.984)
  Pallas kernels: 121 us -> 119 us
    pallas_call x1, Pallas kernels: 121 us -> 119 us  [device_fn(): pl.pallas_call(functools.partial(fused_kernel, n_dev, scale), out_shape=(...]
where the time goes in v7:
time: 122 us; the launch traced here: 121 us
  Pallas kernels  119 us (98%)
  local copies, waits for them, and re-layouts  2.46 us (2%)
    pallas_call x1, Pallas kernels, device_fn(): pl.pallas_call(functools.partial(fused_kernel, n_dev, scale), out_shape=(...  119 us
    unnamed x1, local copies, waits for them, and re-layouts  2.46 us

profile of v7, /device:TPU:21, one launch (start us, length us, event | category | flops | bytes accessed | tf_op | source)
XLA Modules:
  0.0 121.5 jit_solution(15123219838132504484)
XLA Ops:
  0.0 119.0 %fused.1 = (bf16[128,5120]{1,0:T(8,128)(2,1)}, bf16[30,512,1024]{2,1,0:T(8,128)(2,1)}) custom-call(bf16[128,5120]{1,0:T(8,128)(2,1)} %x_ref.1, bf16[128,5120]{1,0:T(8,128)(2,1)} %dy_ref.1, bf16[5120,32,128]{2,1,0:T(8,128)(2,1)} %wq.1, bf16[5120,8,128]{2,1,0:T(8,128)(2,1)} %wk.1, bf16[5120,8,128]{2,1,0:T(8,128)(2,1)} %wv.1, bf16[4096,5120]{1,0:T(8,128)(2,1)} %bitcast.1), custom_call_target="tpu_custom_call" | custom-call | tf_op jit(solution)/shard_map/fused/pallas_call | solution.py:566
  119.0 2.5 %copy.8 = bf16[128,5120]{1,0:T(8,128)(2,1)} copy(bf16[128,5120]{1,0:T(8,128)(2,1)} %get-tuple-element.6) | data formatting | bytes 2621440
